TPU v7x, 512 devices: a whole 4x8x8 slice. The times are simulated.
512 devices in a mesh: tm: 128 (over y, z, core), group: 4 (over x).
Axes of the slice: x: 4, y: 8, z: 8, core: 2. Of those that a mesh axis runs over, the one named last changes fastest.
Arguments:
- values: float32 [1048576, 64], P(('tm', 'group')), may hold values from -6 to 6
- group_ids: int32 [1048576], P(('tm', 'group')), may hold values from 0 to 2047, as said below
- slot_of: int32 [2048], replicated, may hold values from 0 to 2047, each once
Outputs:
- running_mean: float32 [1048576, 64], P(('tm', 'group'))
- running_count: int32 [1048576], P(('tm', 'group'))
- closing_mean: float32 [2048, 64], P('group')
Inputs may be any that keep to these rules, and one draw needn't show every extreme that they name: `slot_of`: a permutation of the slots; slot s belongs to index s // (2048 / 4) of the group axis. `group_ids`: some store groups may have no rows in the window.
All inputs are finite; a program needn't handle non-finite values.
Results may differ from a plain program's by a relative error of at most 0.0003.
Values sent between devices are 32-bit elements; how exact they have to be, the bound alone decides.
No kernel may reach another device: no remote copies, remote signals or barrier semaphores. Data moves between devices by JAX's collectives and lax.ppermute only.
A program may use at most 64 MiB of HBM per device.

v0:
```python
import math

import jax
import jax.numpy as jnp
from jax import lax
from jax.sharding import Mesh
from jax.sharding import PartitionSpec as P

TM = ("tm_0", "tm_1", "tm_2")
TM_GROUP = ("tm_0", "tm_1", "tm_2", "group")


def side_by_side(arrays, axis, split_dim, concat_dim, along):
    columns = [a.reshape(*a.shape[:along], -1) for a in arrays]
    both = jnp.concatenate(columns, axis=along)
    result, at, finished = (
        lax.all_to_all(both, axis, split_axis=split_dim, concat_axis=concat_dim, tiled=True),
        0,
        [],
    )
    for a, column in zip(arrays, columns):
        slab = result[..., at : at + column.shape[along]]
        finished.append(slab.reshape(*slab.shape[:along], *a.shape[along:]))
        at += column.shape[along]
    return tuple(finished)


def nothing_yet(shard, identity):
    return jax.tree.map(
        lambda part, zero: jnp.zeros_like(part) + jnp.asarray(zero, part.dtype), shard, identity
    )


def entering(shard, axes, combine, identity):
    before = start = nothing_yet(shard, identity)
    running = shard
    for axis in reversed(axes):
        devices, mine = (lax.axis_size(axis), lax.axis_index(axis))
        pieces = jax.tree.map(lambda part: lax.all_gather(part, axis), running)
        inside, running = (start, start)
        for k in range(devices):
            passed = k < mine
            running = combine(running, jax.tree.map(lambda part: part[k], pieces))
            inside = jax.tree.map(lambda new, old: jnp.where(passed, new, old), running, inside)
        before = combine(inside, before)
    return before


def rows_for(lines, devices):
    spare = -lines.shape[0] % devices
    if not spare:
        return lines
    return jnp.concatenate([lines, jnp.zeros((spare, *lines.shape[1:]), lines.dtype)])


def from_everyone(shard, axis):
    devices = lax.axis_size(axis)
    return lax.all_to_all(
        jnp.broadcast_to(shard[None], (devices, *shard.shape)), axis, 0, 0, tiled=True
    )


def joined_along(parts, dim):
    shape = list(parts.shape[1:])
    shape[dim] *= parts.shape[0]
    return jnp.moveaxis(parts, 0, dim).reshape(shape)


def gathered_by_axis(shard, axes, dim):
    far, near = axes
    parts = from_everyone(from_everyone(shard, far), near)
    return joined_along(parts.swapaxes(0, 1).reshape(-1, *shard.shape), dim)


def cut_along(shard, dim, devices):
    before, after = (shard.shape[:dim], shard.shape[dim + 1 :])
    return jnp.moveaxis(shard.reshape(*before, devices, -1, *after), dim, 0)


def summed_on_arrival(shard, axis, dim):
    parts = cut_along(shard, dim, lax.axis_size(axis))
    arrived = lax.all_to_all(parts, axis, split_axis=0, concat_axis=0, tiled=True)
    return arrived.sum(axis=0)


def sum_in_two_steps(shard, axes, dim):
    far, near = axes
    parts = cut_along(shard, dim, lax.axis_size(far))
    nearer = summed_on_arrival(parts, near, dim + 1)
    arrived = lax.all_to_all(nearer, far, split_axis=0, concat_axis=0, tiled=True)
    return arrived.sum(axis=0)


def nested_sum(shard, axes):
    padded = rows_for(shard, lax.axis_size(axes[0]) * lax.axis_size(axes[1]))
    whole = gathered_by_axis(sum_in_two_steps(padded, axes, 0), axes, 0)
    return lax.slice_in_dim(whole, 0, len(shard)).reshape(shard.shape)


def in_one(arrays, axis):
    line, at, finished = (jnp.concatenate([a.reshape(-1) for a in arrays]), 0, [])
    running = nested_sum(line, axis)
    for a in arrays:
        finished.append(running[at : at + a.size].reshape(a.shape))
        at += a.size
    return tuple(finished)


def block_totals(values, slots, groups):
    total_rows, width = values.shape
    size = math.gcd(total_rows, 512)
    blocks = total_rows // size
    labels = jnp.arange(groups, dtype=jnp.int32)

    def collect(carry, item):
        rows, keys = item
        onehot = (keys[:, None] == labels[None, :]).astype(jnp.float32)
        sums = lax.dot_general(
            onehot,
            rows,
            (((0,), (0,)), ((), ())),
            precision=lax.Precision.HIGHEST,
            preferred_element_type=jnp.float32,
        )
        return (carry, (sums, jnp.sum(onehot, axis=0)))

    _, stacked = lax.scan(
        collect,
        jnp.zeros((), jnp.float32),
        (values.reshape(blocks, size, width), slots.reshape(blocks, size)),
    )
    return (stacked[0], stacked[1])


def running_pass(values, slots, sums, counts, block_sums, block_counts):
    total_rows, width = values.shape
    blocks = block_sums.shape[0]
    size = total_rows // blocks
    lower = jnp.arange(size)[:, None] >= jnp.arange(size)[None, :]

    def advance(carry, item):
        state, tallies = carry
        rows, keys, add_sums, add_counts = item
        mask = ((keys[:, None] == keys[None, :]) & lower).astype(jnp.float32)
        within = jnp.dot(
            mask, rows, precision=lax.Precision.HIGHEST, preferred_element_type=jnp.float32
        )
        inclusive = within + jnp.take(state, keys, axis=0)
        tally = jnp.sum(mask, axis=1) + jnp.take(tallies, keys)
        return ((state + add_sums, tallies + add_counts), (inclusive, tally))

    items = (
        values.reshape(blocks, size, width),
        slots.reshape(blocks, size),
        block_sums,
        block_counts,
    )
    _, outs = lax.scan(advance, (sums, counts), items)
    return (outs[0].reshape(total_rows, width), outs[1].reshape(total_rows))


def add_pair(earlier, later):
    return (earlier[0] + later[0], earlier[1] + later[1])


def carries(local_sums, local_counts):
    groups, width = local_sums.shape
    owners = lax.axis_size("group")
    per_owner = groups // owners
    zero_block = (jnp.zeros((per_owner, width), jnp.float32), jnp.zeros((per_owner,), jnp.float32))
    arrived_sums, arrived_counts = side_by_side(
        (local_sums.reshape(owners, per_owner, width), local_counts.reshape(owners, per_owner)),
        "group",
        0,
        0,
        2,
    )
    slice_sums = jnp.sum(arrived_sums, axis=0)
    slice_counts = jnp.sum(arrived_counts, axis=0)
    inner_sums = jnp.cumsum(arrived_sums, axis=0) - arrived_sums
    inner_counts = jnp.cumsum(arrived_counts, axis=0) - arrived_counts
    chain_sums, chain_counts = entering((slice_sums, slice_counts), TM, add_pair, zero_block)
    closing_sums, closing_counts = in_one((slice_sums, slice_counts), (("tm_0", "tm_1"), "tm_2"))
    back_sums, back_counts = (
        lax.all_to_all(
            chain_sums[None] + inner_sums, "group", split_axis=0, concat_axis=0, tiled=True
        ),
        lax.all_to_all(
            chain_counts[None] + inner_counts, "group", split_axis=0, concat_axis=0, tiled=True
        ),
    )
    start_sums = back_sums.reshape(groups, width)
    start_counts = back_counts.reshape(groups)
    return (start_sums, start_counts, closing_sums, closing_counts)


def local(values, group_ids, slot_of):
    groups = slot_of.shape[0]
    slots = jnp.take(slot_of, group_ids)
    block_sums, block_counts = block_totals(values, slots, groups)
    local_sums = jnp.sum(block_sums, axis=0)
    local_counts = jnp.sum(block_counts, axis=0)
    start_sums, start_counts, closing_sums, closing_counts = carries(local_sums, local_counts)
    running_sum, count = running_pass(
        values, slots, start_sums, start_counts, block_sums, block_counts
    )
    running_mean = running_sum / count[:, None]
    closing_mean = closing_sums / jnp.maximum(closing_counts, 1.0)[:, None]
    return (running_mean, count.astype(jnp.int32), closing_mean)


def solution(mesh):
    split = Mesh(
        mesh.devices.reshape(8, 8, 2, mesh.shape["group"]), ("tm_0", "tm_1", "tm_2", "group")
    )
    in_specs = (P(TM_GROUP, None), P(TM_GROUP), P())
    out_specs = (P(TM_GROUP, None), P(TM_GROUP), P("group", None))
    return jax.shard_map(local, mesh=split, in_specs=in_specs, out_specs=out_specs, check_vma=False)
```

profile of v0, /device:TPU:1, one launch (start us, length us, event | category | flops | bytes accessed | tf_op | source)
XLA Modules:
  0.0 261.3 jit_solution(1378314662585190917)
XLA Ops:
  7.2 2.4 copy.43
  9.6 0.7 fusion.32
  10.3 11.8 %gather_fusion.2 = s32[2048]{0:T(1024)S(1)} fusion(s32[2048]{0:T(1024)S(1)} %copy-done, s32[2048]{0:T(1024)S(1)} %fusion.32), kind=kCustom, calls=%fused_computation.2 | custom fusion | bytes 24576 | tf_op jit(solution)/shard_map/jit(_take)/gather | solution.py:199
  22.1 13.8 %while.30 = (s32[]{:T(128)}, f32[4,2048,64]{1,2,0:T(8,128)S(1)}, f32[4,2048]{1,0:T(4,128)S(1)}, s32[4,512]{1,0:T(4,128)S(1)}, f32[4,512,64]{2,1,0:T(8,128)}, /*index=5*/s32[]{:T(128)}, s32[]{:T(128)}) while((s32[]{:T(128)}, f32[4,2048,64]{1,2,0:T(8,128)S(1)}, f32[4,2048]{1,0:T(4,128)S(1)}, s32[4,512]{1,0:T(4,128)S(1)}, ...), condition=%wide.region_2.3_spmd.clone, body=%wide.region_0.0_spmd.clone.sunk | while | flops 809498624 | bytes 820309 | solution.py:127
  22.2 2.7 %fusion.52 = f32[4,2048,64]{1,2,0:T(8,128)S(1)} fusion(f32[4,2048,64]{1,2,0:T(8,128)S(1)} %get-tuple-element.316, s32[]{:T(128)} %get-tuple-element.315, s32[512]{0:T(512)S(1)} %bitcast.191, f32[4,512,64]{2,1,0:T(8,128)} %get-tuple-element.326), kind=kOutput, calls=%fused_computation.10.clone.1 | convolution fusion | flops 806354944 | bytes 789504 | tf_op jit(solution)/shard_map/while/body/eval_jaxpr/dot_general | solution.py:118
  24.9 0.6 fusion.53
  25.6 2.7 %fusion.52 = f32[4,2048,64]{1,2,0:T(8,128)S(1)} fusion(f32[4,2048,64]{1,2,0:T(8,128)S(1)} %get-tuple-element.316, s32[]{:T(128)} %get-tuple-element.315, s32[512]{0:T(512)S(1)} %bitcast.191, f32[4,512,64]{2,1,0:T(8,128)} %get-tuple-element.326), kind=kOutput, calls=%fused_computation.10.clone.1 | convolution fusion | flops 806354944 | bytes 789504 | tf_op jit(solution)/shard_map/while/body/eval_jaxpr/dot_general | solution.py:118
  28.3 0.6 fusion.53
  29.1 2.7 %fusion.52 = f32[4,2048,64]{1,2,0:T(8,128)S(1)} fusion(f32[4,2048,64]{1,2,0:T(8,128)S(1)} %get-tuple-element.316, s32[]{:T(128)} %get-tuple-element.315, s32[512]{0:T(512)S(1)} %bitcast.191, f32[4,512,64]{2,1,0:T(8,128)} %get-tuple-element.326), kind=kOutput, calls=%fused_computation.10.clone.1 | convolution fusion | flops 806354944 | bytes 789504 | tf_op jit(solution)/shard_map/while/body/eval_jaxpr/dot_general | solution.py:118
  31.8 0.6 fusion.53
  32.5 2.7 %fusion.52 = f32[4,2048,64]{1,2,0:T(8,128)S(1)} fusion(f32[4,2048,64]{1,2,0:T(8,128)S(1)} %get-tuple-element.316, s32[]{:T(128)} %get-tuple-element.315, s32[512]{0:T(512)S(1)} %bitcast.191, f32[4,512,64]{2,1,0:T(8,128)} %get-tuple-element.326), kind=kOutput, calls=%fused_computation.10.clone.1 | convolution fusion | flops 806354944 | bytes 789504 | tf_op jit(solution)/shard_map/while/body/eval_jaxpr/dot_general | solution.py:118
  35.3 0.6 fusion.53
  36.2 0.4 reshape.141
  36.7 0.6 copy-done.1
  37.5 11.9 %all_to_all.41 = f32[4,512,65]{1,2,0:T(8,128)S(1)} all-to-all(f32[4,512,65]{1,2,0:T(8,128)S(1)} %copy.44), channel_id=1, replica_groups=mesh['tm_0'=8,'tm_1'=8,'tm_2'=2,'group'=4] {'group'}, dimensions={0} | all-to-all | bytes 1064960 | tf_op jit(solution)/shard_map/all_to_all | solution.py:17
  49.5 7.4 %all-gather = f32[1024,64]{0,1:T(8,128)S(1)} all-gather(f32[512,64]{0,1:T(8,128)S(1)} %slice_reduce_fusion), channel_id=2, replica_groups=mesh['tm_0'=8,'tm_1'=8,'tm_2'=2,'group'=4] {'tm_2'}, dimensions={0}, use_global_device_ids=true | all-gather | bytes 393216 | tf_op jit(solution)/shard_map/all_gather | solution.py:39
  56.8 0.7 slice_add_fusion.12
  57.6 38.0 %all-gather.12.cloned.1.call-done = f32[4096,64]{0,1:T(8,128)} async-done(((f32[512,64]{0,1:T(8,128)}), f32[4096,64]{0,1:T(8,128)}) %all-gather.12.cloned.1.call-update) | async-done | bytes 1048592 | tf_op jit(solution)/shard_map/all_gather | solution.py:39
  95.6 2.0 fusion.27
  98.3 8.9 %all_to_all.42 = f32[2,64,260]{2,1,0:T(8,128)S(1)} all-to-all(f32[2,64,260]{2,1,0:T(8,128)S(1)} %copy.52), channel_id=1, replica_groups=mesh['tm_0'=8,'tm_1'=8,'tm_2'=2,'group'=4] {'tm_2'}, dimensions={0} | all-to-all | bytes 266240 | tf_op jit(solution)/shard_map/all_to_all | solution.py:82
  107.2 0.7 all_to_all.30
  107.9 9.7 %all-to-all-start.4 = ((f32[64,1,260]{2,1,0:T(1,128)}), f32[64,1,260]{2,1,0:T(1,128)S(1)}, u32[]{:S(2)}, u32[]{:S(2)}) async-start(f32[64,1,260]{2,1,0:T(1,128)} %all_to_all.30), calls=%async_computation.4 | async-start | bytes 196608 | tf_op jit(solution)/shard_map/all_to_all | solution.py:90
  117.7 2.1 all-gather.4
  119.8 20.3 %all-gather.5 = f32[8,1,512]{2,1,0:T(1,128)S(1)} all-gather(f32[1,1,512]{2,1,0:T(1,128)S(1)} %slice_add_fusion.19), channel_id=5, replica_groups=mesh['tm_0'=8,'tm_1'=8,'tm_2'=2,'group'=4] {'tm_1'}, dimensions={0}, use_global_device_ids=true | all-gather | bytes 18432 | tf_op jit(solution)/shard_map/all_gather | solution.py:39
  140.1 17.8 %all-gather.6 = f32[8,1,512]{2,1,0:T(1,128)S(1)} all-gather(f32[1,1,512]{2,1,0:T(1,128)S(1)} %bitcast.195), channel_id=1, replica_groups=mesh['tm_0'=8,'tm_1'=8,'tm_2'=2,'group'=4] {'tm_0'}, dimensions={0}, use_global_device_ids=true | all-gather | bytes 18432 | tf_op jit(solution)/shard_map/all_gather | solution.py:39
  158.0 0.7 broadcast_in_dim.87
  158.7 7.1 %all-to-all-start.5 = ((f32[64,1,260]{2,1,0:T(1,128)}), f32[64,1,260]{2,1,0:T(1,128)S(1)}, u32[]{:S(2)}, u32[]{:S(2)}) async-start(f32[64,1,260]{2,1,0:T(1,128)} %broadcast_in_dim.87), calls=%async_computation.5 | async-start | bytes 196608 | tf_op jit(solution)/shard_map/all_to_all | solution.py:58
  165.8 11.2 %all-to-all-done.5 = f32[64,1,260]{2,1,0:T(1,128)S(1)} async-done(((f32[64,1,260]{2,1,0:T(1,128)}), f32[64,1,260]{2,1,0:T(1,128)S(1)}, u32[]{:S(2)}, u32[]{:S(2)}) %all-to-all-start.5) | async-done | bytes 66592 | tf_op jit(solution)/shard_map/all_to_all | solution.py:58
  177.1 0.7 broadcast_in_dim.89
  177.7 14.5 %all-to-all-start.6 = ((f32[2,64,260]{2,1,0:T(8,128)}), f32[2,64,260]{2,1,0:T(8,128)S(1)}, u32[]{:S(2)}, u32[]{:S(2)}) async-start(f32[2,64,260]{2,1,0:T(8,128)} %broadcast_in_dim.89), calls=%async_computation.6 | async-start | bytes 393216 | tf_op jit(solution)/shard_map/all_to_all | solution.py:58
  192.3 1.6 fusion.26
  193.8 0.8 fusion.22
  194.7 4.0 %all-to-all-start.1 = ((f32[4,512,64]{1,2,0:T(8,128)}), f32[4,512,64]{1,2,0:T(8,128)S(1)}, u32[]{:S(2)}, u32[]{:S(2)}) async-start(f32[4,512,64]{1,2,0:T(8,128)} %fusion.22), calls=%async_computation.1 | async-start | bytes 1048576 | tf_op jit(solution)/shard_map/all_to_all | solution.py:185
  198.7 0.6 copy.47
  200.0 7.9 %all-to-all-done.1 = f32[4,512,64]{1,2,0:T(8,128)S(1)} async-done(((f32[4,512,64]{1,2,0:T(8,128)}), f32[4,512,64]{1,2,0:T(8,128)S(1)}, u32[]{:S(2)}, u32[]{:S(2)}) %all-to-all-start.1) | async-done | bytes 524320 | tf_op jit(solution)/shard_map/all_to_all | solution.py:185
  207.9 3.4 %all-to-all-start.2 = ((f32[4,1,512]{2,1,0:T(1,128)}), f32[4,1,512]{2,1,0:T(1,128)S(1)}, u32[]{:S(2)}, u32[]{:S(2)}) async-start(f32[4,1,512]{2,1,0:T(1,128)} %copy.47), calls=%async_computation.2 | async-start | bytes 16384 | tf_op jit(solution)/shard_map/all_to_all | solution.py:188
  211.5 0.8 copy.55
  212.6 2.7 %all-to-all-done.2 = f32[4,1,512]{2,1,0:T(1,128)S(1)} async-done(((f32[4,1,512]{2,1,0:T(1,128)}), f32[4,1,512]{2,1,0:T(1,128)S(1)}, u32[]{:S(2)}, u32[]{:S(2)}) %all-to-all-start.2) | async-done | bytes 8224 | tf_op jit(solution)/shard_map/all_to_all | solution.py:188
  215.3 37.6 %while.31 = (s32[]{:T(128)}, f32[2048,64]{1,0:T(8,128)S(1)}, f32[2048]{0:T(1024)S(1)}, f32[4,512,64]{1,0,2:T(4,128)S(1)}, f32[4,512]{1,0:T(4,128)S(1)}, /*index=...) while((s32[]{:T(128)}, f32[2048,64]{1,0:T(8,128)S(1)}, ...), condition=%wide.region_11.12_spmd.clone, body=%wide.region_9.11_spmd.clone.sunk | while | flops 203631616 | bytes 5328513 | solution.py:158
  215.3 1.0 gather_fusion
  216.5 1.6 fusion.56
  218.2 1.3 dynamic_update_slice.27
  219.7 3.1 %gather_fusion.1 = f32[512]{0:T(512)S(1)} fusion(f32[2048]{0:T(1024)S(1)} %get-tuple-element.342, s32[1024]{0:T(1024)S(1)} %pad_clamp_fusion.2), kind=kCustom, calls=%fused_computation.1.clone.clone.1 | custom fusion | bytes 6144 | tf_op jit(solution)/shard_map/while/body/eval_jaxpr/jit(_take)/gather | solution.py:149
  223.0 1.1 constant_dynamic-slice_fusion.9
  224.0 0.3 copy.83
  224.7 1.0 gather_fusion
  225.9 1.6 fusion.56
  227.6 1.3 dynamic_update_slice.27
  229.1 3.1 %gather_fusion.1 = f32[512]{0:T(512)S(1)} fusion(f32[2048]{0:T(1024)S(1)} %get-tuple-element.342, s32[1024]{0:T(1024)S(1)} %pad_clamp_fusion.2), kind=kCustom, calls=%fused_computation.1.clone.clone.1 | custom fusion | bytes 6144 | tf_op jit(solution)/shard_map/while/body/eval_jaxpr/jit(_take)/gather | solution.py:149
  232.4 1.1 constant_dynamic-slice_fusion.9
  233.5 0.3 copy.83
  234.1 1.0 gather_fusion
  235.3 1.6 fusion.56
  237.0 1.3 dynamic_update_slice.27
  238.6 3.1 %gather_fusion.1 = f32[512]{0:T(512)S(1)} fusion(f32[2048]{0:T(1024)S(1)} %get-tuple-element.342, s32[1024]{0:T(1024)S(1)} %pad_clamp_fusion.2), kind=kCustom, calls=%fused_computation.1.clone.clone.1 | custom fusion | bytes 6144 | tf_op jit(solution)/shard_map/while/body/eval_jaxpr/jit(_take)/gather | solution.py:149
  241.8 1.1 constant_dynamic-slice_fusion.9
  242.9 0.3 copy.83
  243.5 1.0 gather_fusion
  244.7 1.6 fusion.56
  246.4 1.3 dynamic_update_slice.27
  248.0 3.1 %gather_fusion.1 = f32[512]{0:T(512)S(1)} fusion(f32[2048]{0:T(1024)S(1)} %get-tuple-element.342, s32[1024]{0:T(1024)S(1)} %pad_clamp_fusion.2), kind=kCustom, calls=%fused_computation.1.clone.clone.1 | custom fusion | bytes 6144 | tf_op jit(solution)/shard_map/while/body/eval_jaxpr/jit(_take)/gather | solution.py:149
  251.2 1.1 constant_dynamic-slice_fusion.9
  253.1 0.6 convert_element_type.9
  253.7 0.8 broadcast_divide_fusion
  (104 shorter events, 7.0 us)
Async XLA Ops:
  7.2 3.2 %copy-start = (s32[2048]{0:T(1024)S(1)}, s32[2048]{0:T(1024)}, u32[]{:S(2)}) copy-start(s32[2048]{0:T(1024)} %param.9) | copy-start | bytes 24580
  7.2 88.4 %all-gather.12.cloned.1.call-start = ((), (), s32[]{:S(2)}) async-start(), calls=%async_computation.8 | async-start | bytes 1179648 | tf_op jit(solution)/shard_map/all_gather | solution.py:39
  10.3 11.8 %copy-start.4 = (s32[2048]{0:T(1024)S(1)}, s32[2048]{0:T(1024)}, u32[]{:S(2)}) copy-start(s32[2048]{0:T(1024)} %param.8) | copy-start | bytes 24580
  36.0 1.4 copy-start.1
  57.5 134.7 %all-gather.10.cloned.1.call-start = ((), (), s32[]{:S(2)}) async-start(), calls=%async_computation.7 | async-start | bytes 1179648 | tf_op jit(solution)/shard_map/all_gather | solution.py:39
  97.7 94.6 %copy-start.2 = (f32[4096,64]{0,1:T(8,128)S(1)}, f32[4096,64]{0,1:T(8,128)}, u32[]{:S(2)}) copy-start(f32[4096,64]{0,1:T(8,128)} %all-gather.12.cloned.1.call-done) | copy-start | bytes 3145732
  97.7 94.6 %copy-start.3 = (f32[1,512,64]{1,2,0:T(8,128)S(1)}, f32[1,512,64]{1,2,0:T(8,128)}, u32[]{:S(2)}) copy-start(f32[1,512,64]{1,2,0:T(8,128)} %get-tuple-element.214) | copy-start | bytes 393220
  107.9 50.0 %all-to-all-start.4 = ((f32[64,1,260]{2,1,0:T(1,128)}), f32[64,1,260]{2,1,0:T(1,128)S(1)}, u32[]{:S(2)}, u32[]{:S(2)}) async-start(f32[64,1,260]{2,1,0:T(1,128)} %all_to_all.30), calls=%async_computation.4 | async-start | bytes 196608 | tf_op jit(solution)/shard_map/all_to_all | solution.py:90
  158.7 18.3 %all-to-all-start.5 = ((f32[64,1,260]{2,1,0:T(1,128)}), f32[64,1,260]{2,1,0:T(1,128)S(1)}, u32[]{:S(2)}, u32[]{:S(2)}) async-start(f32[64,1,260]{2,1,0:T(1,128)} %broadcast_in_dim.87), calls=%async_computation.5 | async-start | bytes 196608 | tf_op jit(solution)/shard_map/all_to_all | solution.py:58
  177.7 16.9 %all-to-all-start.6 = ((f32[2,64,260]{2,1,0:T(8,128)}), f32[2,64,260]{2,1,0:T(8,128)S(1)}, u32[]{:S(2)}, u32[]{:S(2)}) async-start(f32[2,64,260]{2,1,0:T(8,128)} %broadcast_in_dim.89), calls=%async_computation.6 | async-start | bytes 393216 | tf_op jit(solution)/shard_map/all_to_all | solution.py:58
  194.7 13.2 %all-to-all-start.1 = ((f32[4,512,64]{1,2,0:T(8,128)}), f32[4,512,64]{1,2,0:T(8,128)S(1)}, u32[]{:S(2)}, u32[]{:S(2)}) async-start(f32[4,512,64]{1,2,0:T(8,128)} %fusion.22), calls=%async_computation.1 | async-start | bytes 1048576 | tf_op jit(solution)/shard_map/all_to_all | solution.py:185
  207.9 7.4 %all-to-all-start.2 = ((f32[4,1,512]{2,1,0:T(1,128)}), f32[4,1,512]{2,1,0:T(1,128)S(1)}, u32[]{:S(2)}, u32[]{:S(2)}) async-start(f32[4,1,512]{2,1,0:T(1,128)} %copy.47), calls=%async_computation.2 | async-start | bytes 16384 | tf_op jit(solution)/shard_map/all_to_all | solution.py:188
Sparse Core Ops, SparseCore 0:
  57.7 37.8 all-gather.11
  98.2 39.2 all-gather.9
where the time goes:
time: 262 us; the launch traced here: 261 us
  blocking collectives  68.4 us (26%)
  waiting for transfers between devices  59.8 us (23%)
  local copies, waits for them, and re-layouts  49.7 us (19%)
  starting transfers between devices  38.8 us (15%)
  matrix products  17.3 us (7%)
  between operations  14.4 us (5%)
  other arithmetic  12.3 us (5%)
    all_gather x4, blocking collectives, entering(): pieces = jax.tree.map(lambda part: lax.all_gather(part, axis), running)  47.6 us
    all_gather x2, waiting for transfers between devices, entering(): pieces = jax.tree.map(lambda part: lax.all_gather(part, axis), running)  38 us
    all_to_all x2, starting transfers between devices, from_everyone(): lax.all_to_all(jnp.broadcast_to(shard[None], (devices, *shard.shape)), ax...  21.6 us
    gather x4, local copies, waits for them, and re-layouts, advance(): tally = jnp.sum(mask, axis=1) + jnp.take(tallies, keys)  12.6 us
    all_to_all x1, blocking collectives, side_by_side(): lax.all_to_all(both, axis, split_axis=split_dim, concat_axis=concat_dim,...  11.9 us
    gather x1, local copies, waits for them, and re-layouts, local(): slots = jnp.take(slot_of, group_ids)  11.8 us
    all_to_all x2, waiting for transfers between devices, from_everyone(): lax.all_to_all(jnp.broadcast_to(shard[None], (devices, *shard.shape)), ax...  11.2 us
    dot_general x4, matrix products, collect(): lax.dot_general(onehot, rows, (((0,), (0,)), ((), ())), precision=lax.Pre...  10.9 us
  transfers between devices with their start and end apart: 7, of which 4 were waited for; matrix products, arithmetic and copies ran while one was open for 3% of the time, Pallas kernels for 0%

commit v1 on v0

v1 whole, which is shorter than its diff:
```python
import jax
import jax.numpy as jnp
from jax import lax
from jax.experimental import pallas as pl
from jax.experimental.pallas import tpu as pltpu
from jax.sharding import Mesh
from jax.sharding import PartitionSpec as P

ROWS_ALL = ("y", "z", "c", "x")
F32 = jnp.float32
BF16 = jnp.bfloat16
M = 64
R = 2048
S = 2048
LANES = 128
T = 256
NT = S // T
SIB = 8
FAR = 64
MSG = 136
LHS = 208


def pieces(v):
    a = v.astype(BF16)
    rest = v - a.astype(F32)
    b = rest.astype(BF16)
    c = (rest - b.astype(F32)).astype(BF16)
    return a, b, c


def lookup(table, idx):
    low = jnp.bitwise_and(idx, LANES - 1)
    high = jnp.right_shift(idx, 7)
    out = jnp.zeros_like(idx)
    for k in range(S // LANES):
        row = jnp.broadcast_to(table[k : k + 1, :], idx.shape)
        out = jnp.where(high == k, jnp.take_along_axis(row, low, axis=1), out)
    return out


def columns(slot):
    flipped = jnp.concatenate([slot] * 8, axis=0).T
    return [jnp.broadcast_to(flipped[:, i : i + 1], (LANES, LANES)) for i in range(R // LANES)]


def dot(a, b):
    return lax.dot_general(a, b, (((1,), (0,)), ((), ())), preferred_element_type=F32)


def sums_kernel(vt, gid, table, out, slot_out, cols, left, hot):
    slot = lookup(table[...], gid[...])
    slot_out[...] = slot
    for i, block in enumerate(columns(slot)):
        cols[i * LANES : (i + 1) * LANES, :] = block
    a, b, c = pieces(vt[...])
    left[0:64, :] = a
    left[64:128, :] = b
    left[128:192, :] = c
    left[192:208, :] = jnp.ones((16, R), BF16)
    lane = lax.broadcasted_iota(jnp.int32, (R, LANES), 1)
    first = lax.broadcasted_iota(jnp.int32, (8, LANES), 0) == 0

    def tile(j, carry):
        keys = cols[...] - lane
        for h in range(2):
            hot[:, h * LANES : (h + 1) * LANES] = jnp.where(
                keys == j * T + h * LANES, 1.0, 0.0
            ).astype(BF16)
        res = dot(left[...], hot[...])
        total = res[0:64] + (res[64:128] + res[128:192])
        out[j, 0:64, :] = total[:, :LANES]
        out[j, 64:128, :] = total[:, LANES:]
        out[j, 128:136, :] = jnp.where(first, res[192:200, :LANES], res[192:200, LANES:])
        return carry

    lax.fori_loop(0, NT, tile, 0)


def slice_kernel(arrived, out, buf):
    total = arrived[0]
    for i in range(1, SIB):
        total = total + arrived[i]
    buf[...] = total
    counts = buf[128:130, :]
    for p in range(FAR):
        out[p, 0:2, :] = buf[2 * p : 2 * p + 2, :]
        out[p, 2:4, :] = counts


def scan_kernel(place, arrived, out, counts_out):
    mine = place[0]
    acc = jnp.zeros((4, LANES), F32)
    before = jnp.zeros((4, LANES), F32)
    for p in range(FAR):
        got = arrived[p]
        out[p, 0:2, :] = acc[0:2]
        before = before + jnp.where(p < mine, got, 0.0)
        acc = acc + got
    number = jnp.where(mine < FAR // 2, acc[2:3], acc[3:4])
    closing = acc[0:2] / jnp.maximum(number, 1.0)
    for p in range(FAR):
        out[p, 2:4, :] = closing
    counts_out[0:2, :] = before[2:4]


def start_kernel(far, arrived, counts, out, closing, buf):
    for p in range(FAR):
        buf[2 * p : 2 * p + 2, :] = far[p, 0:2, :]
        closing[2 * p : 2 * p + 2, :] = far[p, 2:4, :]
    buf[128:130, :] = counts[0:2, :]
    buf[130:136, :] = jnp.zeros((6, LANES), F32)
    acc = buf[...]
    for k in range(SIB):
        i = 2 * (k % 4) + k // 4
        out[i] = acc
        acc = acc + arrived[i]


def running_kernel(start, vt, slot, closed, mean, count, closing, cols, left, local, hot, same):
    for i, block in enumerate(columns(slot[...])):
        cols[i * LANES : (i + 1) * LANES, :] = block
    a, b, c = pieces(vt[...])
    local[0:64, :] = a
    local[64:128, :] = b
    local[128:192, :] = c
    sub = lax.broadcasted_iota(jnp.int32, (16, R), 0)
    local[192:208, :] = jnp.where(sub == 0, 1.0, 0.0).astype(BF16)
    sub = lax.broadcasted_iota(jnp.int32, (16, LANES), 0)
    for j in range(NT):
        for h in range(2):
            at = slice(j * T + h * LANES, j * T + (h + 1) * LANES)
            a, b, c = pieces(start[j, h * 64 : (h + 1) * 64, :])
            left[0:64, at] = a
            left[64:128, at] = b
            left[128:192, at] = c
            a, b, c = (
                jnp.broadcast_to(v.astype(F32), (16, LANES))
                for v in pieces(start[j, 128 + h : 129 + h, :])
            )
            left[192:208, at] = jnp.where(
                sub == 0, a, jnp.where(sub == 1, b, jnp.where(sub == 2, c, 0.0))
            ).astype(BF16)
    for j in range(NT):
        upto = (j + 1) * T
        for h in range(2):
            i = 2 * j + h
            at = slice(h * LANES, (h + 1) * LANES)
            row = slot[i : i + 1, :]
            label = lax.broadcasted_iota(jnp.int32, (S, LANES), 0)
            hot[:, at] = jnp.where(label == row, 1.0, 0.0).astype(BF16)
            eq = cols[0:upto, :] == row
            if j:
                same[0 : j * T, at] = jnp.where(eq[0 : j * T], 1.0, 0.0).astype(BF16)
            q = lax.broadcasted_iota(jnp.int32, (T, LANES), 0)
            r = lax.broadcasted_iota(jnp.int32, (T, LANES), 1) + h * LANES
            last = jnp.logical_and(cols[j * T : upto, :] == row, q <= r)
            same[j * T : upto, at] = jnp.where(last, 1.0, 0.0).astype(BF16)
        res = dot(left[...], hot[...]) + dot(local[:, 0:upto], same[0:upto, :])
        total = res[0:64] + (res[64:128] + res[128:192])
        tally = (res[192:193] + res[193:194]) + res[194:195]
        mean[:, j * T : upto] = total / tally
        whole = tally.astype(jnp.int32)
        count[2 * j : 2 * j + 1, :] = whole[:, :LANES]
        count[2 * j + 1 : 2 * j + 2, :] = whole[:, LANES:]
    for c in range(2):
        for h in range(2):
            closing[:, c * T + h * LANES : c * T + (h + 1) * LANES] = closed[c, h * 64 : (h + 1) * 64, :]


def shape(*dims, dtype=F32):
    return jax.ShapeDtypeStruct(dims, dtype)


def sums_call(vt, gid, table):
    return pl.pallas_call(
        sums_kernel,
        out_shape=(shape(SIB, MSG, LANES), shape(16, LANES, dtype=jnp.int32)),
        scratch_shapes=[
            pltpu.VMEM((R, LANES), jnp.int32),
            pltpu.VMEM((LHS, R), BF16),
            pltpu.VMEM((R, T), BF16),
        ],
        name="local_sums",
    )(vt, gid, table)


def running_call(start, vt, slot, closed):
    return pl.pallas_call(
        running_kernel,
        out_shape=(shape(M, R), shape(16, LANES, dtype=jnp.int32), shape(M, 512)),
        scratch_shapes=[
            pltpu.VMEM((R, LANES), jnp.int32),
            pltpu.VMEM((LHS, S), BF16),
            pltpu.VMEM((LHS, R), BF16),
            pltpu.VMEM((S, T), BF16),
            pltpu.VMEM((R, T), BF16),
        ],
        name="running_means",
    )(start, vt, slot, closed)


def local(values, group_ids, slot_of):
    vt = values.T
    gid = group_ids.reshape(16, LANES)
    table = slot_of.reshape(16, LANES)
    sums, slot = sums_call(vt, gid, table)
    siblings = ("x", "c")
    far = ("y", "z")
    arrived = lax.all_to_all(sums, siblings, 0, 0, tiled=True)
    pieces_out = pl.pallas_call(
        slice_kernel,
        out_shape=shape(FAR, 4, LANES),
        scratch_shapes=[pltpu.VMEM((MSG, LANES), F32)],
        name="slice_sums",
    )(arrived)
    met = lax.all_to_all(pieces_out, far, 0, 0, tiled=True)
    place = (lax.axis_index("y") * 8 + lax.axis_index("z")).astype(jnp.int32).reshape(1)
    scanned, counts = pl.pallas_call(
        scan_kernel,
        in_specs=[
            pl.BlockSpec(memory_space=pltpu.SMEM),
            pl.BlockSpec(memory_space=pltpu.VMEM),
        ],
        out_shape=(shape(FAR, 4, LANES), shape(8, LANES)),
        name="scan",
    )(place, met)
    back = lax.all_to_all(scanned, far, 0, 0, tiled=True)
    starts, closing_half = pl.pallas_call(
        start_kernel,
        out_shape=(shape(SIB, MSG, LANES), shape(LANES, LANES)),
        scratch_shapes=[pltpu.VMEM((MSG, LANES), F32)],
        name="starts",
    )(back, arrived, counts)
    closed = lax.all_gather(closing_half, "c")
    start = lax.all_to_all(starts, siblings, 0, 0, tiled=True)
    mean, count, closing = running_call(start, vt, slot, closed)
    return mean.T, count.reshape(R), closing.T


def solution(mesh):
    split = Mesh(mesh.devices.reshape(8, 8, 2, 4), ROWS_ALL)
    in_specs = (P(ROWS_ALL, None), P(ROWS_ALL), P())
    out_specs = (P(ROWS_ALL, None), P(ROWS_ALL), P("x", None))
    return jax.shard_map(local, mesh=split, in_specs=in_specs, out_specs=out_specs, check_vma=False)
```

time: 262 us -> 101 us (0.39)
  local copies, waits for them, and re-layouts: 49.7 us -> 1.47 us
  waiting for transfers between devices: 59.8 us -> 19.2 us
  blocking collectives: 68.4 us -> 40.2 us
  Pallas kernels: 0 us -> 21.1 us
  starting transfers between devices: 38.8 us -> 17.9 us
  matrix products: 17.3 us -> 0 us
  between operations: 14.4 us -> 0.65 us
  other arithmetic: 12.3 us -> 0 us
    all_gather x4 -> x1, blocking collectives: 47.6 us -> 2.02 us  [local(): closed = lax.all_gather(closing_half, 'c')]
    all_gather x2 -> x0, waiting for transfers between devices: 38 us -> none  [entering(): pieces = jax.tree.map(lambda part: lax.all_gather(part, axis), running)]
    gather x13 -> x0, local copies, waits for them, and re-layouts: 28.9 us -> none  [the longest x4 12.6 us: advance(): tally = jnp.sum(mask, axis=1) + jnp.take(tallies, keys)]
    pallas_call x0 -> x5, Pallas kernels: none -> 21.1 us  [the longest x1 8.3 us: running_call(): pl.pallas_call(running_kernel, out_shape=(shape(M, R), shape(16, LANES, d...]
    all_to_all x5 -> x2, starting transfers between devices: 38.7 us -> 17.9 us  [the longest x1 11.2 us: local(): met = lax.all_to_all(pieces_out, far, 0, 0, tiled=True)]
    all_to_all x2, blocking collectives: 20.8 us -> 38.2 us  [the longest x1 21.2 us: local(): arrived = lax.all_to_all(sums, siblings, 0, 0, tiled=True)]
    dot_general x8 -> x0, matrix products: 17.3 us -> none  [the longest x4 10.9 us: collect(): lax.dot_general(onehot, rows, (((0,), (0,)), ((), ())), precision=lax.Pre...]
    dynamic_update_slice x16 -> x0, local copies, waits for them, and re-layouts: 6.28 us -> none  [the longest x12 5.76 us: running_pass(): _, outs = lax.scan(advance, (sums, counts), items)]
  transfers between devices with their start and end apart: 7 -> 2, of which waited for: 4 -> 2; matrix products, arithmetic and copies ran while one was open for 3% -> 0% of each run, Pallas kernels for 0% -> 0%
where the time goes in v1:
time: 101 us; the launch traced here: 100 us
  blocking collectives  40.2 us (40%)
  Pallas kernels  21.1 us (21%)
  waiting for transfers between devices  19.2 us (19%)
  starting transfers between devices  17.9 us (18%)
  local copies, waits for them, and re-layouts  1.47 us (1%)
    all_to_all x1, blocking collectives, local(): arrived = lax.all_to_all(sums, siblings, 0, 0, tiled=True)  21.2 us
    all_to_all x1, blocking collectives, local(): back = lax.all_to_all(scanned, far, 0, 0, tiled=True)  17 us
    all_to_all x1, waiting for transfers between devices, local(): met = lax.all_to_all(pieces_out, far, 0, 0, tiled=True)  11.5 us
    all_to_all x1, starting transfers between devices, local(): met = lax.all_to_all(pieces_out, far, 0, 0, tiled=True)  11.2 us
    pallas_call x1, Pallas kernels, running_call(): pl.pallas_call(running_kernel, out_shape=(shape(M, R), shape(16, LANES, d...  8.3 us
    all_to_all x1, waiting for transfers between devices, local(): start = lax.all_to_all(starts, siblings, 0, 0, tiled=True)  7.71 us
    pallas_call x1, Pallas kernels, sums_call(): pl.pallas_call(sums_kernel, out_shape=(shape(SIB, MSG, LANES), shape(16,...  7.37 us
    all_to_all x1, starting transfers between devices, local(): start = lax.all_to_all(starts, siblings, 0, 0, tiled=True)  6.72 us
  transfers between devices with their start and end apart: 2, of which 2 were waited for; matrix products, arithmetic and copies ran while one was open for 0% of the time, Pallas kernels for 0%

profile of v1, /device:TPU:1, one launch (start us, length us, event | category | flops | bytes accessed | tf_op | source)
XLA Modules:
  0.0 100.5 jit_solution(9501246949851710021)
XLA Ops:
  0.6 7.4 %local_sums.1 = (f32[8,136,128]{2,1,0:T(8,128)}, s32[16,128]{1,0:T(8,128)}) custom-call(f32[64,2048]{1,0:T(8,128)} %bitcast.8, s32[16,128]{1,0:T(8,128)} %bitcast.11, s32[16,128]{1,0:T(8,128)} %bitcast.12), custom_call_target="tpu_custom_call" | custom-call | tf_op jit(solution)/shard_map/local_sums/pallas_call | solution.py:176
  8.0 21.2 %all_to_all.20.arrived = f32[8,136,128]{2,1,0:T(8,128)} all-to-all(f32[8,136,128]{2,1,0:T(8,128)} %get-tuple-element.12), channel_id=1, replica_groups=mesh['y'=8,'z'=8,'c'=2,'x'=4] {'x','c'}, dimensions={0} | all-to-all | bytes 1114112 | tf_op jit(solution)/shard_map/all_to_all | solution.py:210
  29.2 1.8 %slice_sums.1 = f32[64,4,128]{2,1,0:T(4,128)} custom-call(f32[8,136,128]{2,1,0:T(8,128)} %all_to_all.20.arrived), custom_call_target="tpu_custom_call" | custom-call | tf_op jit(solution)/shard_map/slice_sums/pallas_call | solution.py:211
  30.9 11.2 %all-to-all-start.1 = ((f32[64,4,128]{2,1,0:T(4,128)}), f32[64,4,128]{2,1,0:T(4,128)S(1)}, u32[]{:S(2)}, u32[]{:S(2)}) async-start(f32[64,4,128]{2,1,0:T(4,128)} %slice_sums.1), calls=%async_computation.1 | async-start | bytes 262144 | tf_op jit(solution)/shard_map/all_to_all | solution.py:217
  42.1 11.5 %all-to-all-done.1.arrived = f32[64,4,128]{2,1,0:T(4,128)S(1)} async-done(((f32[64,4,128]{2,1,0:T(4,128)}), f32[64,4,128]{2,1,0:T(4,128)S(1)}, u32[]{:S(2)}, u32[]{:S(2)}) %all-to-all-start.1) | async-done | bytes 131104 | tf_op jit(solution)/shard_map/all_to_all | solution.py:217
  53.6 0.0 copy-start.1
  53.6 0.7 copy-done.1
  54.3 1.7 %scan.1 = (f32[64,4,128]{2,1,0:T(4,128)}, f32[8,128]{1,0:T(8,128)}) custom-call(s32[1]{0:T(128)} %bitcast.place, f32[64,4,128]{2,1,0:T(4,128)} %copy-done.1), custom_call_target="tpu_custom_call" | custom-call | tf_op jit(solution)/shard_map/scan/pallas_call | solution.py:219
  55.9 17.0 %all_to_all.21.far = f32[64,4,128]{2,1,0:T(4,128)} all-to-all(f32[64,4,128]{2,1,0:T(4,128)} %get-tuple-element.13), channel_id=1, replica_groups=mesh['y'=8,'z'=8,'c'=2,'x'=4] {'y','z'}, dimensions={0} | all-to-all | bytes 262144 | tf_op jit(solution)/shard_map/all_to_all | solution.py:228
  73.0 2.0 %starts.1 = (f32[8,136,128]{2,1,0:T(8,128)}, f32[128,128]{1,0:T(8,128)}) custom-call(f32[64,4,128]{2,1,0:T(4,128)} %all_to_all.21.far, f32[8,136,128]{2,1,0:T(8,128)} %all_to_all.20.arrived, f32[8,128]{1,0:T(8,128)} %get-tuple-element.14.counts), custom_call_target="tpu_custom_call" | custom-call | tf_op jit(solution)/shard_map/starts/pallas_call | solution.py:229
  74.9 0.0 copy-start.2
  74.9 6.7 %all-to-all-start.3 = ((f32[8,136,128]{2,1,0:T(8,128)}), f32[8,136,128]{2,1,0:T(8,128)S(1)}, u32[]{:S(2)}, u32[]{:S(2)}) async-start(f32[8,136,128]{2,1,0:T(8,128)} %get-tuple-element.15), calls=%async_computation.3 | async-start | bytes 1114112 | tf_op jit(solution)/shard_map/all_to_all | solution.py:236
  81.7 0.0 copy-done.2
  81.7 2.0 %all-gather = f32[256,128]{1,0:T(8,128)} all-gather(f32[128,128]{1,0:T(8,128)S(1)} %copy-done.2), channel_id=2, replica_groups=mesh['y'=8,'z'=8,'c'=2,'x'=4] {'c'}, dimensions={0}, use_global_device_ids=true | all-gather | bytes 196608 | tf_op jit(solution)/shard_map/all_gather | solution.py:235
  83.7 7.7 %all-to-all-done.3.start = f32[8,136,128]{2,1,0:T(8,128)S(1)} async-done(((f32[8,136,128]{2,1,0:T(8,128)}), f32[8,136,128]{2,1,0:T(8,128)S(1)}, u32[]{:S(2)}, u32[]{:S(2)}) %all-to-all-start.3) | async-done | bytes 557088 | tf_op jit(solution)/shard_map/all_to_all | solution.py:236
  91.4 0.0 copy-start
  91.4 0.8 copy-done
  92.2 8.3 %running_means.1 = (f32[64,2048]{1,0:T(8,128)}, s32[16,128]{1,0:T(8,128)}, f32[64,512]{1,0:T(8,128)}) custom-call(f32[8,136,128]{2,1,0:T(8,128)} %copy-done, f32[64,2048]{1,0:T(8,128)} %bitcast.9, s32[16,128]{1,0:T(8,128)} %get-tuple-element.16.slot, f32[2,128,128]{2,1,0:T(8,128)} %bitcast.10), custom_call_target="tpu_custom_call" | custom-call | tf_op jit(solution)/shard_map/running_means/pallas_call | solution.py:189
Async XLA Ops:
  30.9 22.7 %all-to-all-start.1 = ((f32[64,4,128]{2,1,0:T(4,128)}), f32[64,4,128]{2,1,0:T(4,128)S(1)}, u32[]{:S(2)}, u32[]{:S(2)}) async-start(f32[64,4,128]{2,1,0:T(4,128)} %slice_sums.1), calls=%async_computation.1 | async-start | bytes 262144 | tf_op jit(solution)/shard_map/all_to_all | solution.py:217
  53.6 0.7 copy-start.1
  74.9 6.7 %copy-start.2 = (f32[128,128]{1,0:T(8,128)S(1)}, f32[128,128]{1,0:T(8,128)}, u32[]{:S(2)}) copy-start(f32[128,128]{1,0:T(8,128)} %get-tuple-element.17) | copy-start | bytes 196612
  74.9 16.5 %all-to-all-start.3 = ((f32[8,136,128]{2,1,0:T(8,128)}), f32[8,136,128]{2,1,0:T(8,128)S(1)}, u32[]{:S(2)}, u32[]{:S(2)}) async-start(f32[8,136,128]{2,1,0:T(8,128)} %get-tuple-element.15), calls=%async_computation.3 | async-start | bytes 1114112 | tf_op jit(solution)/shard_map/all_to_all | solution.py:236
  91.4 0.8 copy-start

commit v2 on v1

--- a/solution.py
+++ b/solution.py
@@ -88,8 +88,8 @@
         out[p, 2:4, :] = counts
 
 
-def scan_kernel(place, arrived, out, counts_out):
-    mine = place[0]
+def scan_kernel(arrived, out, counts_out):
+    mine = lax.axis_index("y") * 8 + lax.axis_index("z")
     acc = jnp.zeros((4, LANES), F32)
     before = jnp.zeros((4, LANES), F32)
     for p in range(FAR):
@@ -172,10 +172,18 @@
     return jax.ShapeDtypeStruct(dims, dtype)
 
 
+def near(*dims, dtype=F32):
+    return pltpu.VMEM(dims, dtype)
+
+
+def held(x):
+    return pltpu.with_memory_space_constraint(x, pltpu.VMEM)
+
+
 def sums_call(vt, gid, table):
     return pl.pallas_call(
         sums_kernel,
-        out_shape=(shape(SIB, MSG, LANES), shape(16, LANES, dtype=jnp.int32)),
+        out_shape=(near(SIB, MSG, LANES), near(16, LANES, dtype=jnp.int32)),
         scratch_shapes=[
             pltpu.VMEM((R, LANES), jnp.int32),
             pltpu.VMEM((LHS, R), BF16),
@@ -207,33 +215,30 @@
     sums, slot = sums_call(vt, gid, table)
     siblings = ("x", "c")
     far = ("y", "z")
-    arrived = lax.all_to_all(sums, siblings, 0, 0, tiled=True)
+    arrived = held(lax.all_to_all(sums, siblings, 0, 0, tiled=True))
     pieces_out = pl.pallas_call(
         slice_kernel,
-        out_shape=shape(FAR, 4, LANES),
+        out_shape=near(FAR, 4, LANES),
         scratch_shapes=[pltpu.VMEM((MSG, LANES), F32)],
         name="slice_sums",
     )(arrived)
-    met = lax.all_to_all(pieces_out, far, 0, 0, tiled=True)
-    place = (lax.axis_index("y") * 8 + lax.axis_index("z")).astype(jnp.int32).reshape(1)
+    met = held(lax.all_to_all(pieces_out, far, 0, 0, tiled=True))
     scanned, counts = pl.pallas_call(
         scan_kernel,
-        in_specs=[
-            pl.BlockSpec(memory_space=pltpu.SMEM),
-            pl.BlockSpec(memory_space=pltpu.VMEM),
-        ],
-        out_shape=(shape(FAR, 4, LANES), shape(8, LANES)),
+        out_shape=(near(FAR, 4, LANES), near(8, LANES)),
         name="scan",
-    )(place, met)
-    back = lax.all_to_all(scanned, far, 0, 0, tiled=True)
+    )(met)
+    back = held(lax.all_to_all(scanned, far, 0, 0, tiled=True))
     starts, closing_half = pl.pallas_call(
         start_kernel,
-        out_shape=(shape(SIB, MSG, LANES), shape(LANES, LANES)),
+        out_shape=(near(SIB, MSG, LANES), near(LANES, LANES)),
         scratch_shapes=[pltpu.VMEM((MSG, LANES), F32)],
         name="starts",
     )(back, arrived, counts)
     closed = lax.all_gather(closing_half, "c")
-    start = lax.all_to_all(starts, siblings, 0, 0, tiled=True)
+    starts, closed = lax.optimization_barrier((starts, closed))
+    closed = held(closed)
+    start = held(lax.all_to_all(starts, siblings, 0, 0, tiled=True))
     mean, count, closing = running_call(start, vt, slot, closed)
     return mean.T, count.reshape(R), closing.T
 

time: 101 us -> 92.9 us (0.920)
  blocking collectives: 40.2 us -> 76.3 us
  waiting for transfers between devices: 19.2 us -> 0 us
  starting transfers between devices: 17.9 us -> 0 us
  Pallas kernels: 21.1 us -> 15.6 us
  local copies, waits for them, and re-layouts: 1.47 us -> 0.01 us
    all_to_all x2 -> x4, blocking collectives: 38.2 us -> 71.6 us  [the longest x1 24 us: local(): met = held(lax.all_to_all(pieces_out, far, 0, 0, tiled=True))]
    all_to_all x2 -> x0, waiting for transfers between devices: 19.2 us -> none  [the longest x1 11.5 us: local(): met = lax.all_to_all(pieces_out, far, 0, 0, tiled=True)]
    all_to_all x2 -> x0, starting transfers between devices: 17.9 us -> none  [the longest x1 11.2 us: local(): met = lax.all_to_all(pieces_out, far, 0, 0, tiled=True)]
    pallas_call x4, Pallas kernels: 12.8 us -> 7.48 us  [the longest x1 6.55 us: sums_call(): pl.pallas_call(sums_kernel, out_shape=(near(SIB, MSG, LANES), near(16, LA...]
    all_gather x1, blocking collectives: 2.02 us -> 4.7 us  [local(): closed = lax.all_gather(closing_half, 'c')]
    unnamed x6 -> x4, local copies, waits for them, and re-layouts: 1.47 us -> 0.01 us
  transfers between devices with their start and end apart: 2 -> 0, of which waited for: 2 -> 0; matrix products, arithmetic and copies ran while one was open for 0% -> 0% of each run, Pallas kernels for 0% -> 0%
where the time goes in v2:
time: 92.9 us; the launch traced here: 92.6 us
  blocking collectives  76.3 us (82%)
  Pallas kernels  15.6 us (17%)
    all_to_all x1, blocking collectives, local(): met = held(lax.all_to_all(pieces_out, far, 0, 0, tiled=True))  24 us
    all_to_all x1, blocking collectives, local(): arrived = held(lax.all_to_all(sums, siblings, 0, 0, tiled=True))  19.4 us
    all_to_all x1, blocking collectives, local(): back = held(lax.all_to_all(scanned, far, 0, 0, tiled=True))  15.4 us
    all_to_all x1, blocking collectives, local(): start = held(lax.all_to_all(starts, siblings, 0, 0, tiled=True))  12.9 us
    pallas_call x1, Pallas kernels, running_call(): pl.pallas_call(running_kernel, out_shape=(shape(M, R), shape(16, LANES, d...  8.1 us
    pallas_call x1, Pallas kernels, sums_call(): pl.pallas_call(sums_kernel, out_shape=(near(SIB, MSG, LANES), near(16, LA...  6.55 us
    all_gather x1, blocking collectives, local(): closed = lax.all_gather(closing_half, 'c')  4.7 us

profile of v2, /device:TPU:1, one launch (start us, length us, event | category | flops | bytes accessed | tf_op | source)
XLA Modules:
  0.0 92.6 jit_solution(13744499897869417990)
XLA Ops:
  0.6 6.6 %local_sums.1 = (f32[8,136,128]{2,1,0:T(8,128)S(1)}, s32[16,128]{1,0:T(8,128)S(1)}) custom-call(f32[64,2048]{1,0:T(8,128)} %bitcast.8, s32[16,128]{1,0:T(8,128)} %bitcast.10, s32[16,128]{1,0:T(8,128)} %bitcast.11), custom_call_target="tpu_custom_call" | custom-call | tf_op jit(solution)/shard_map/local_sums/pallas_call | solution.py:184
  7.2 0.0 copy-start
  7.2 19.4 %all_to_all.20.arrived = f32[8,136,128]{2,1,0:T(8,128)S(1)} all-to-all(f32[8,136,128]{2,1,0:T(8,128)S(1)} %get-tuple-element.14), channel_id=1, replica_groups=mesh['y'=8,'z'=8,'c'=2,'x'=4] {'x','c'}, dimensions={0} | all-to-all | bytes 1114112 | tf_op jit(solution)/shard_map/all_to_all | solution.py:218
  26.6 0.0 copy-done
  26.6 0.1 slice_sums.1
  26.6 24.0 %all_to_all.21.arrived = f32[64,4,128]{2,1,0:T(4,128)S(1)} all-to-all(f32[64,4,128]{2,1,0:T(4,128)S(1)} %slice_sums.1), channel_id=1, replica_groups=mesh['y'=8,'z'=8,'c'=2,'x'=4] {'y','z'}, dimensions={0} | all-to-all | bytes 262144 | tf_op jit(solution)/shard_map/all_to_all | solution.py:225
  50.6 0.1 scan.1
  50.7 0.0 copy-start.1
  50.7 15.4 %all_to_all.22.far = f32[64,4,128]{2,1,0:T(4,128)S(1)} all-to-all(f32[64,4,128]{2,1,0:T(4,128)S(1)} %get-tuple-element.15), channel_id=1, replica_groups=mesh['y'=8,'z'=8,'c'=2,'x'=4] {'y','z'}, dimensions={0} | all-to-all | bytes 262144 | tf_op jit(solution)/shard_map/all_to_all | solution.py:231
  66.2 0.0 copy-done.1
  66.2 0.8 starts.1
  66.9 4.7 %all-gather = f32[256,128]{1,0:T(8,128)S(1)} all-gather(f32[128,128]{1,0:T(8,128)S(1)} %get-tuple-element.18), channel_id=2, replica_groups=mesh['y'=8,'z'=8,'c'=2,'x'=4] {'c'}, dimensions={0}, use_global_device_ids=true | all-gather | bytes 196608 | tf_op jit(solution)/shard_map/all_gather | solution.py:238
  71.6 12.9 %all_to_all.23.start = f32[8,136,128]{2,1,0:T(8,128)S(1)} all-to-all(f32[8,136,128]{2,1,0:T(8,128)S(1)} %get-tuple-element.19), channel_id=1, replica_groups=mesh['y'=8,'z'=8,'c'=2,'x'=4] {'x','c'}, dimensions={0} | all-to-all | bytes 1114112 | tf_op jit(solution)/shard_map/all_to_all | solution.py:241
  84.5 8.1 %running_means.1 = (f32[64,2048]{1,0:T(8,128)}, s32[16,128]{1,0:T(8,128)}, f32[64,512]{1,0:T(8,128)}) custom-call(f32[8,136,128]{2,1,0:T(8,128)S(1)} %all_to_all.23.start, f32[64,2048]{1,0:T(8,128)} %bitcast.9, s32[16,128]{1,0:T(8,128)} %copy-done, f32[2,128,128]{2,1,0:T(8,128)S(1)} %bitcast.7), custom_call_target="tpu_custom_call" | custom-call | tf_op jit(solution)/shard_map/running_means/pallas_call | solution.py:197
Async XLA Ops:
  7.2 19.4 %copy-start = (s32[16,128]{1,0:T(8,128)}, s32[16,128]{1,0:T(8,128)S(1)}, u32[]{:S(2)}) copy-start(s32[16,128]{1,0:T(8,128)S(1)} %get-tuple-element.20.slot) | copy-start | bytes 24580
  50.7 15.5 %copy-start.1 = (f32[8,128]{1,0:T(8,128)}, f32[8,128]{1,0:T(8,128)S(1)}, u32[]{:S(2)}) copy-start(f32[8,128]{1,0:T(8,128)S(1)} %get-tuple-element.16.counts) | copy-start | bytes 12292

commit v3 on v2

--- a/solution.py
+++ b/solution.py
@@ -21,6 +21,9 @@
 LHS = 208
 
 
+ROOM = pltpu.CompilerParams(vmem_limit_bytes=16 << 20)
+
+
 def pieces(v):
     a = v.astype(BF16)
     rest = v - a.astype(F32)
@@ -48,33 +51,45 @@
     return lax.dot_general(a, b, (((1,), (0,)), ((), ())), preferred_element_type=F32)
 
 
-def sums_kernel(vt, gid, table, out, slot_out, cols, left, hot):
+def hot(mask):
+    return jnp.where(mask, 1.0, 0.0).astype(BF16)
+
+
+def sums_kernel(vt_far, gid_far, table_far, out, slot_out, local, cols, vt, gid, table, sems):
+    values_in = pltpu.make_async_copy(vt_far, vt, sems.at[0])
+    keys_in = pltpu.make_async_copy(gid_far, gid, sems.at[1])
+    table_in = pltpu.make_async_copy(table_far, table, sems.at[2])
+    keys_in.start()
+    table_in.start()
+    values_in.start()
+    keys_in.wait()
+    table_in.wait()
     slot = lookup(table[...], gid[...])
     slot_out[...] = slot
     for i, block in enumerate(columns(slot)):
         cols[i * LANES : (i + 1) * LANES, :] = block
+    values_in.wait()
     a, b, c = pieces(vt[...])
-    left[0:64, :] = a
-    left[64:128, :] = b
-    left[128:192, :] = c
-    left[192:208, :] = jnp.ones((16, R), BF16)
-    lane = lax.broadcasted_iota(jnp.int32, (R, LANES), 1)
+    local[0:64, :] = a
+    local[64:128, :] = b
+    local[128:192, :] = c
+    sub = lax.broadcasted_iota(jnp.int32, (16, R), 0)
+    local[192:208, :] = jnp.where(sub == 0, 1.0, 0.0).astype(BF16)
+    lane = lax.broadcasted_iota(jnp.int32, (T, T), 1)
     first = lax.broadcasted_iota(jnp.int32, (8, LANES), 0) == 0
-
-    def tile(j, carry):
-        keys = cols[...] - lane
-        for h in range(2):
-            hot[:, h * LANES : (h + 1) * LANES] = jnp.where(
-                keys == j * T + h * LANES, 1.0, 0.0
-            ).astype(BF16)
-        res = dot(left[...], hot[...])
+    for j in range(NT):
+        res = None
+        for k in range(NT):
+            at = slice(k * T, (k + 1) * T)
+            keys = cols[at, :]
+            keys = jnp.concatenate([keys, keys], axis=1)
+            part = dot(local[:, at], hot(keys == lane + j * T))
+            res = part if res is None else res + part
         total = res[0:64] + (res[64:128] + res[128:192])
         out[j, 0:64, :] = total[:, :LANES]
         out[j, 64:128, :] = total[:, LANES:]
-        out[j, 128:136, :] = jnp.where(first, res[192:200, :LANES], res[192:200, LANES:])
-        return carry
-
-    lax.fori_loop(0, NT, tile, 0)
+        number = jnp.broadcast_to(res[192:193], (8, T))
+        out[j, 128:136, :] = jnp.where(first, number[:, :LANES], number[:, LANES:])
 
 
 def slice_kernel(arrived, out, buf):
@@ -117,15 +132,7 @@
         acc = acc + arrived[i]
 
 
-def running_kernel(start, vt, slot, closed, mean, count, closing, cols, left, local, hot, same):
-    for i, block in enumerate(columns(slot[...])):
-        cols[i * LANES : (i + 1) * LANES, :] = block
-    a, b, c = pieces(vt[...])
-    local[0:64, :] = a
-    local[64:128, :] = b
-    local[128:192, :] = c
-    sub = lax.broadcasted_iota(jnp.int32, (16, R), 0)
-    local[192:208, :] = jnp.where(sub == 0, 1.0, 0.0).astype(BF16)
+def running_kernel(start, local, slot, cols, closed, mean, count, closing, left, held_mean, sems):
     sub = lax.broadcasted_iota(jnp.int32, (16, LANES), 0)
     for j in range(NT):
         for h in range(2):
@@ -141,31 +148,37 @@
             left[192:208, at] = jnp.where(
                 sub == 0, a, jnp.where(sub == 1, b, jnp.where(sub == 2, c, 0.0))
             ).astype(BF16)
+    label = lax.broadcasted_iota(jnp.int32, (T, T), 0)
+    order = label <= lax.broadcasted_iota(jnp.int32, (T, T), 1)
+    copies = []
     for j in range(NT):
-        upto = (j + 1) * T
-        for h in range(2):
-            i = 2 * j + h
-            at = slice(h * LANES, (h + 1) * LANES)
-            row = slot[i : i + 1, :]
-            label = lax.broadcasted_iota(jnp.int32, (S, LANES), 0)
-            hot[:, at] = jnp.where(label == row, 1.0, 0.0).astype(BF16)
-            eq = cols[0:upto, :] == row
-            if j:
-                same[0 : j * T, at] = jnp.where(eq[0 : j * T], 1.0, 0.0).astype(BF16)
-            q = lax.broadcasted_iota(jnp.int32, (T, LANES), 0)
-            r = lax.broadcasted_iota(jnp.int32, (T, LANES), 1) + h * LANES
-            last = jnp.logical_and(cols[j * T : upto, :] == row, q <= r)
-            same[j * T : upto, at] = jnp.where(last, 1.0, 0.0).astype(BF16)
-        res = dot(left[...], hot[...]) + dot(local[:, 0:upto], same[0:upto, :])
+        row = jnp.concatenate([slot[2 * j : 2 * j + 1, :], slot[2 * j + 1 : 2 * j + 2, :]], axis=1)
+        row = jnp.broadcast_to(row, (T, T))
+        res = None
+        for k in range(NT):
+            part = dot(left[:, k * T : (k + 1) * T], hot(label + k * T == row))
+            res = part if res is None else res + part
+        for k in range(j + 1):
+            at = slice(k * T, (k + 1) * T)
+            keys = cols[at, :]
+            mask = jnp.concatenate([keys, keys], axis=1) == row
+            if k == j:
+                mask = jnp.logical_and(mask, order)
+            res = res + dot(local[:, at], hot(mask))
         total = res[0:64] + (res[64:128] + res[128:192])
         tally = (res[192:193] + res[193:194]) + res[194:195]
-        mean[:, j * T : upto] = total / tally
+        at = slice(j * T, (j + 1) * T)
+        held_mean[:, at] = total / tally
+        copies.append(pltpu.make_async_copy(held_mean.at[:, at], mean.at[:, at], sems.at[j]))
+        copies[-1].start()
         whole = tally.astype(jnp.int32)
         count[2 * j : 2 * j + 1, :] = whole[:, :LANES]
         count[2 * j + 1 : 2 * j + 2, :] = whole[:, LANES:]
     for c in range(2):
         for h in range(2):
             closing[:, c * T + h * LANES : c * T + (h + 1) * LANES] = closed[c, h * 64 : (h + 1) * 64, :]
+    for copy in copies:
+        copy.wait()
 
 
 def shape(*dims, dtype=F32):
@@ -176,43 +189,57 @@
     return pltpu.VMEM(dims, dtype)
 
 
+def outer(x):
+    return pltpu.with_memory_space_constraint(x, pltpu.HBM)
+
+
 def held(x):
     return pltpu.with_memory_space_constraint(x, pltpu.VMEM)
 
 
 def sums_call(vt, gid, table):
+    outside = pl.BlockSpec(memory_space=pl.ANY)
     return pl.pallas_call(
         sums_kernel,
-        out_shape=(near(SIB, MSG, LANES), near(16, LANES, dtype=jnp.int32)),
+        in_specs=[outside] * 3,
+        out_shape=(
+            near(SIB, MSG, LANES),
+            near(16, LANES, dtype=jnp.int32),
+            near(LHS, R, dtype=BF16),
+            near(R, LANES, dtype=jnp.int32),
+        ),
         scratch_shapes=[
-            pltpu.VMEM((R, LANES), jnp.int32),
-            pltpu.VMEM((LHS, R), BF16),
-            pltpu.VMEM((R, T), BF16),
+            pltpu.VMEM((M, R), F32),
+            pltpu.VMEM((16, LANES), jnp.int32),
+            pltpu.VMEM((16, LANES), jnp.int32),
+            pltpu.SemaphoreType.DMA((3,)),
         ],
+        compiler_params=ROOM,
         name="local_sums",
-    )(vt, gid, table)
-
-
-def running_call(start, vt, slot, closed):
+    )(outer(vt), outer(gid), outer(table))
+
+
+def running_call(start, local, slot, cols, closed):
+    vmem = pl.BlockSpec(memory_space=pltpu.VMEM)
     return pl.pallas_call(
         running_kernel,
         out_shape=(shape(M, R), shape(16, LANES, dtype=jnp.int32), shape(M, 512)),
+        out_specs=(pl.BlockSpec(memory_space=pl.ANY), vmem, vmem),
         scratch_shapes=[
-            pltpu.VMEM((R, LANES), jnp.int32),
             pltpu.VMEM((LHS, S), BF16),
-            pltpu.VMEM((LHS, R), BF16),
-            pltpu.VMEM((S, T), BF16),
-            pltpu.VMEM((R, T), BF16),
+            pltpu.VMEM((M, R), F32),
+            pltpu.SemaphoreType.DMA((NT,)),
         ],
+        compiler_params=ROOM,
         name="running_means",
-    )(start, vt, slot, closed)
+    )(start, held(local), held(slot), held(cols), closed)
 
 
 def local(values, group_ids, slot_of):
     vt = values.T
     gid = group_ids.reshape(16, LANES)
     table = slot_of.reshape(16, LANES)
-    sums, slot = sums_call(vt, gid, table)
+    sums, slot, local_pieces, cols = sums_call(vt, gid, table)
     siblings = ("x", "c")
     far = ("y", "z")
     arrived = held(lax.all_to_all(sums, siblings, 0, 0, tiled=True))
@@ -220,12 +247,14 @@
         slice_kernel,
         out_shape=near(FAR, 4, LANES),
         scratch_shapes=[pltpu.VMEM((MSG, LANES), F32)],
+        compiler_params=ROOM,
         name="slice_sums",
     )(arrived)
     met = held(lax.all_to_all(pieces_out, far, 0, 0, tiled=True))
     scanned, counts = pl.pallas_call(
         scan_kernel,
         out_shape=(near(FAR, 4, LANES), near(8, LANES)),
+        compiler_params=ROOM,
         name="scan",
     )(met)
     back = held(lax.all_to_all(scanned, far, 0, 0, tiled=True))
@@ -233,13 +262,14 @@
         start_kernel,
         out_shape=(near(SIB, MSG, LANES), near(LANES, LANES)),
         scratch_shapes=[pltpu.VMEM((MSG, LANES), F32)],
+        compiler_params=ROOM,
         name="starts",
     )(back, arrived, counts)
     closed = lax.all_gather(closing_half, "c")
     starts, closed = lax.optimization_barrier((starts, closed))
     closed = held(closed)
     start = held(lax.all_to_all(starts, siblings, 0, 0, tiled=True))
-    mean, count, closing = running_call(start, vt, slot, closed)
+    mean, count, closing = running_call(start, local_pieces, slot, cols, closed)
     return mean.T, count.reshape(R), closing.T
 
 

time: 92.9 us -> 85.3 us (0.918)
  Pallas kernels: 15.6 us -> 8.04 us
    pallas_call x1, Pallas kernels: 8.1 us -> 4.52 us  [running_call(): pl.pallas_call(running_kernel, out_shape=(shape(M, R), shape(16, LANES, d...]
    pallas_call x1, Pallas kernels: 6.55 us -> 3.27 us  [sums_call(): pl.pallas_call(sums_kernel, in_specs=[outside] * 3, out_shape=(near(SIB,...]
where the time goes in v3:
time: 85.3 us; the launch traced here: 85 us
  blocking collectives  76.3 us (89%)
  Pallas kernels  8.04 us (9%)
    all_to_all x1, blocking collectives, local(): met = held(lax.all_to_all(pieces_out, far, 0, 0, tiled=True))  24 us
    all_to_all x1, blocking collectives, local(): arrived = held(lax.all_to_all(sums, siblings, 0, 0, tiled=True))  19.4 us
    all_to_all x1, blocking collectives, local(): back = held(lax.all_to_all(scanned, far, 0, 0, tiled=True))  15.4 us
    all_to_all x1, blocking collectives, local(): start = held(lax.all_to_all(starts, siblings, 0, 0, tiled=True))  12.9 us
    all_gather x1, blocking collectives, local(): closed = lax.all_gather(closing_half, 'c')  4.7 us
    pallas_call x1, Pallas kernels, running_call(): pl.pallas_call(running_kernel, out_shape=(shape(M, R), shape(16, LANES, d...  4.52 us
    pallas_call x1, Pallas kernels, sums_call(): pl.pallas_call(sums_kernel, in_specs=[outside] * 3, out_shape=(near(SIB,...  3.27 us

profile of v3, /device:TPU:1, one launch (start us, length us, event | category | flops | bytes accessed | tf_op | source)
XLA Modules:
  0.0 85.0 jit_solution(10264420153355795017)
XLA Ops:
  0.6 3.3 %local_sums.1 = (f32[8,136,128]{2,1,0:T(8,128)S(1)}, s32[16,128]{1,0:T(8,128)S(1)}, bf16[208,2048]{1,0:T(8,128)(2,1)S(1)}, s32[2048,128]{1,0:T(8,128)S(1)}) custom-call(f32[64,2048]{1,0:T(8,128)} %bitcast.8, s32[16,128]{1,0:T(8,128)} %bitcast.9, s32[16,128]{1,0:T(8,128)} %bitcast.10), custom_call_target="tpu_custom_call" | custom-call | tf_op jit(solution)/shard_map/local_sums/pallas_call | solution.py:202
  3.9 19.4 %all_to_all.20.arrived = f32[8,136,128]{2,1,0:T(8,128)S(1)} all-to-all(f32[8,136,128]{2,1,0:T(8,128)S(1)} %get-tuple-element.16), channel_id=1, replica_groups=mesh['y'=8,'z'=8,'c'=2,'x'=4] {'x','c'}, dimensions={0} | all-to-all | bytes 1114112 | tf_op jit(solution)/shard_map/all_to_all | solution.py:245
  23.3 0.1 slice_sums.1
  23.3 24.0 %all_to_all.21.arrived = f32[64,4,128]{2,1,0:T(4,128)S(1)} all-to-all(f32[64,4,128]{2,1,0:T(4,128)S(1)} %slice_sums.1), channel_id=1, replica_groups=mesh['y'=8,'z'=8,'c'=2,'x'=4] {'y','z'}, dimensions={0} | all-to-all | bytes 262144 | tf_op jit(solution)/shard_map/all_to_all | solution.py:253
  47.3 0.1 scan.1
  47.4 15.4 %all_to_all.22.far = f32[64,4,128]{2,1,0:T(4,128)S(1)} all-to-all(f32[64,4,128]{2,1,0:T(4,128)S(1)} %get-tuple-element.17), channel_id=1, replica_groups=mesh['y'=8,'z'=8,'c'=2,'x'=4] {'y','z'}, dimensions={0} | all-to-all | bytes 262144 | tf_op jit(solution)/shard_map/all_to_all | solution.py:260
  62.9 0.1 starts.1
  62.9 4.7 %all-gather = f32[256,128]{1,0:T(8,128)S(1)} all-gather(f32[128,128]{1,0:T(8,128)S(1)} %get-tuple-element.20), channel_id=2, replica_groups=mesh['y'=8,'z'=8,'c'=2,'x'=4] {'c'}, dimensions={0}, use_global_device_ids=true | all-gather | bytes 196608 | tf_op jit(solution)/shard_map/all_gather | solution.py:268
  67.6 12.9 %all_to_all.23.start = f32[8,136,128]{2,1,0:T(8,128)S(1)} all-to-all(f32[8,136,128]{2,1,0:T(8,128)S(1)} %get-tuple-element.21), channel_id=1, replica_groups=mesh['y'=8,'z'=8,'c'=2,'x'=4] {'x','c'}, dimensions={0} | all-to-all | bytes 1114112 | tf_op jit(solution)/shard_map/all_to_all | solution.py:271
  80.5 4.5 %running_means.1 = (f32[64,2048]{1,0:T(8,128)}, s32[16,128]{1,0:T(8,128)}, f32[64,512]{1,0:T(8,128)}) custom-call(f32[8,136,128]{2,1,0:T(8,128)S(1)} %all_to_all.23.start, bf16[208,2048]{1,0:T(8,128)(2,1)S(1)} %get-tuple-element.22.local, s32[16,128]{1,0:T(8,128)S(1)} %get-tuple-element.23.slot, s32[2048,128]{1,0:T(8,128)S(1)} %get-tuple-element.24.cols, ...), custom_call_target="tpu_custom_call" | custom-call | tf_op jit(solution)/shard_map/running_means/pallas_call | solution.py:224

commit v4 on v3

--- a/solution.py
+++ b/solution.py
@@ -16,7 +16,7 @@
 T = 256
 NT = S // T
 SIB = 8
-FAR = 64
+RING = 8
 MSG = 136
 LHS = 208
 
@@ -92,40 +92,50 @@
         out[j, 128:136, :] = jnp.where(first, number[:, :LANES], number[:, LANES:])
 
 
-def slice_kernel(arrived, out, buf):
+def slice_kernel(arrived, out):
     total = arrived[0]
     for i in range(1, SIB):
         total = total + arrived[i]
-    buf[...] = total
-    counts = buf[128:130, :]
-    for p in range(FAR):
-        out[p, 0:2, :] = buf[2 * p : 2 * p + 2, :]
-        out[p, 2:4, :] = counts
-
-
-def scan_kernel(arrived, out, counts_out):
-    mine = lax.axis_index("y") * 8 + lax.axis_index("z")
-    acc = jnp.zeros((4, LANES), F32)
-    before = jnp.zeros((4, LANES), F32)
-    for p in range(FAR):
-        got = arrived[p]
-        out[p, 0:2, :] = acc[0:2]
-        before = before + jnp.where(p < mine, got, 0.0)
-        acc = acc + got
-    number = jnp.where(mine < FAR // 2, acc[2:3], acc[3:4])
-    closing = acc[0:2] / jnp.maximum(number, 1.0)
-    for p in range(FAR):
-        out[p, 2:4, :] = closing
-    counts_out[0:2, :] = before[2:4]
-
-
-def start_kernel(far, arrived, counts, out, closing, buf):
-    for p in range(FAR):
-        buf[2 * p : 2 * p + 2, :] = far[p, 0:2, :]
-        closing[2 * p : 2 * p + 2, :] = far[p, 2:4, :]
-    buf[128:130, :] = counts[0:2, :]
-    buf[130:136, :] = jnp.zeros((6, LANES), F32)
-    acc = buf[...]
+    for p in range(RING):
+        out[p, 0:16, :] = total[16 * p : 16 * p + 16]
+        out[p, 16:24, :] = total[128:136]
+
+
+def ring_kernel(arrived, out):
+    total = arrived[0]
+    for i in range(1, RING):
+        total = total + arrived[i]
+    for p in range(RING):
+        out[p] = total
+
+
+def scan_kernel(arrived, rings, out, counts_out):
+    y = lax.axis_index("y")
+    z = lax.axis_index("z")
+    total = rings[0]
+    before = jnp.where(y > 0, total, 0.0)
+    for i in range(1, RING):
+        ring = rings[i]
+        before = before + jnp.where(i < y, ring, 0.0)
+        total = total + ring
+    number = jnp.where(z < RING // 2, total[16:17], total[17:18])
+    closing = total[0:16] / jnp.maximum(number, 1.0)
+    counts = before[16:24]
+    acc = before[0:16]
+    for p in range(RING):
+        out[p, 0:16, :] = acc
+        out[p, 16:32, :] = closing
+        acc = acc + arrived[p, 0:16, :]
+        counts = counts + jnp.where(p < z, arrived[p, 16:24, :], 0.0)
+    counts_out[...] = counts
+
+
+def start_kernel(far, arrived, counts, out, closing):
+    parts = []
+    for p in range(RING):
+        parts.append(far[p, 0:16, :])
+        closing[16 * p : 16 * p + 16, :] = far[p, 16:32, :]
+    acc = jnp.concatenate(parts + [counts[...]], axis=0)
     for k in range(SIB):
         i = 2 * (k % 4) + k // 4
         out[i] = acc
@@ -241,27 +251,31 @@
     table = slot_of.reshape(16, LANES)
     sums, slot, local_pieces, cols = sums_call(vt, gid, table)
     siblings = ("x", "c")
-    far = ("y", "z")
     arrived = held(lax.all_to_all(sums, siblings, 0, 0, tiled=True))
-    pieces_out = pl.pallas_call(
+    parts = pl.pallas_call(
         slice_kernel,
-        out_shape=near(FAR, 4, LANES),
-        scratch_shapes=[pltpu.VMEM((MSG, LANES), F32)],
+        out_shape=near(RING, 24, LANES),
         compiler_params=ROOM,
         name="slice_sums",
     )(arrived)
-    met = held(lax.all_to_all(pieces_out, far, 0, 0, tiled=True))
+    along_z = held(lax.all_to_all(parts, "z", 0, 0, tiled=True))
+    ring = pl.pallas_call(
+        ring_kernel,
+        out_shape=near(RING, 24, LANES),
+        compiler_params=ROOM,
+        name="ring_sums",
+    )(along_z)
+    along_y = held(lax.all_to_all(ring, "y", 0, 0, tiled=True))
     scanned, counts = pl.pallas_call(
         scan_kernel,
-        out_shape=(near(FAR, 4, LANES), near(8, LANES)),
+        out_shape=(near(RING, 32, LANES), near(8, LANES)),
         compiler_params=ROOM,
         name="scan",
-    )(met)
-    back = held(lax.all_to_all(scanned, far, 0, 0, tiled=True))
+    )(along_z, along_y)
+    back = held(lax.all_to_all(scanned, "z", 0, 0, tiled=True))
     starts, closing_half = pl.pallas_call(
         start_kernel,
         out_shape=(near(SIB, MSG, LANES), near(LANES, LANES)),
-        scratch_shapes=[pltpu.VMEM((MSG, LANES), F32)],
         compiler_params=ROOM,
         name="starts",
     )(back, arrived, counts)

time: 85.3 us -> 85.5 us (level)
    all_gather x1, blocking collectives: 4.7 us -> 6.25 us  [local(): closed = lax.all_gather(closing_half, 'c')]
    all_to_all x2 -> x3, blocking collectives: 39.4 us -> 38.2 us  [the longest x1 14.2 us: local(): along_y = held(lax.all_to_all(ring, 'y', 0, 0, tiled=True))]
where the time goes in v4:
time: 85.5 us; the launch traced here: 85.2 us
  blocking collectives  76.6 us (90%)
  Pallas kernels  7.91 us (9%)
    all_to_all x1, blocking collectives, local(): arrived = held(lax.all_to_all(sums, siblings, 0, 0, tiled=True))  19.4 us
    all_to_all x1, blocking collectives, local(): along_y = held(lax.all_to_all(ring, 'y', 0, 0, tiled=True))  14.2 us
    all_to_all x1, blocking collectives, local(): along_z = held(lax.all_to_all(parts, 'z', 0, 0, tiled=True))  13.7 us
    all_to_all x1, blocking collectives, local(): start = held(lax.all_to_all(starts, siblings, 0, 0, tiled=True))  12.9 us
    all_to_all x1, blocking collectives, local(): back = held(lax.all_to_all(scanned, 'z', 0, 0, tiled=True))  10.3 us
    all_gather x1, blocking collectives, local(): closed = lax.all_gather(closing_half, 'c')  6.25 us
    pallas_call x1, Pallas kernels, running_call(): pl.pallas_call(running_kernel, out_shape=(shape(M, R), shape(16, LANES, d...  4.52 us
    pallas_call x1, Pallas kernels, sums_call(): pl.pallas_call(sums_kernel, in_specs=[outside] * 3, out_shape=(near(SIB,...  3.27 us

profile of v4, /device:TPU:1, one launch (start us, length us, event | category | flops | bytes accessed | tf_op | source)
XLA Modules:
  0.0 85.2 jit_solution(6012543720625347885)
XLA Ops:
  0.6 3.3 %local_sums.1 = (f32[8,136,128]{2,1,0:T(8,128)S(1)}, s32[16,128]{1,0:T(8,128)S(1)}, bf16[208,2048]{1,0:T(8,128)(2,1)S(1)}, s32[2048,128]{1,0:T(8,128)S(1)}) custom-call(f32[64,2048]{1,0:T(8,128)} %bitcast.8, s32[16,128]{1,0:T(8,128)} %bitcast.9, s32[16,128]{1,0:T(8,128)} %bitcast.10), custom_call_target="tpu_custom_call" | custom-call | tf_op jit(solution)/shard_map/local_sums/pallas_call | solution.py:212
  3.9 19.4 %all_to_all.25.arrived = f32[8,136,128]{2,1,0:T(8,128)S(1)} all-to-all(f32[8,136,128]{2,1,0:T(8,128)S(1)} %get-tuple-element.16), channel_id=1, replica_groups=mesh['y'=8,'z'=8,'c'=2,'x'=4] {'x','c'}, dimensions={0} | all-to-all | bytes 1114112 | tf_op jit(solution)/shard_map/all_to_all | solution.py:254
  23.3 13.7 %all_to_all.26.arrived = f32[8,24,128]{2,1,0:T(8,128)S(1)} all-to-all(f32[8,24,128]{2,1,0:T(8,128)S(1)} %slice_sums.1), channel_id=1, replica_groups=mesh['y'=8,'z'=8,'c'=2,'x'=4] {'z'}, dimensions={0} | all-to-all | bytes 196608 | tf_op jit(solution)/shard_map/all_to_all | solution.py:261
  37.0 14.2 %all_to_all.27.rings = f32[8,24,128]{2,1,0:T(8,128)S(1)} all-to-all(f32[8,24,128]{2,1,0:T(8,128)S(1)} %ring_sums.1), channel_id=1, replica_groups=mesh['y'=8,'z'=8,'c'=2,'x'=4] {'y'}, dimensions={0} | all-to-all | bytes 196608 | tf_op jit(solution)/shard_map/all_to_all | solution.py:268
  51.2 10.3 %all_to_all.28.far = f32[8,32,128]{2,1,0:T(8,128)S(1)} all-to-all(f32[8,32,128]{2,1,0:T(8,128)S(1)} %get-tuple-element.17), channel_id=1, replica_groups=mesh['y'=8,'z'=8,'c'=2,'x'=4] {'z'}, dimensions={0} | all-to-all | bytes 262144 | tf_op jit(solution)/shard_map/all_to_all | solution.py:275
  61.6 6.3 %all-gather = f32[256,128]{1,0:T(8,128)S(1)} all-gather(f32[128,128]{1,0:T(8,128)S(1)} %get-tuple-element.20), channel_id=2, replica_groups=mesh['y'=8,'z'=8,'c'=2,'x'=4] {'c'}, dimensions={0}, use_global_device_ids=true | all-gather | bytes 196608 | tf_op jit(solution)/shard_map/all_gather | solution.py:282
  67.8 12.9 %all_to_all.29.start = f32[8,136,128]{2,1,0:T(8,128)S(1)} all-to-all(f32[8,136,128]{2,1,0:T(8,128)S(1)} %get-tuple-element.21), channel_id=1, replica_groups=mesh['y'=8,'z'=8,'c'=2,'x'=4] {'x','c'}, dimensions={0} | all-to-all | bytes 1114112 | tf_op jit(solution)/shard_map/all_to_all | solution.py:285
  80.7 4.5 %running_means.1 = (f32[64,2048]{1,0:T(8,128)}, s32[16,128]{1,0:T(8,128)}, f32[64,512]{1,0:T(8,128)}) custom-call(f32[8,136,128]{2,1,0:T(8,128)S(1)} %all_to_all.29.start, bf16[208,2048]{1,0:T(8,128)(2,1)S(1)} %get-tuple-element.22.local, s32[16,128]{1,0:T(8,128)S(1)} %get-tuple-element.23.slot, s32[2048,128]{1,0:T(8,128)S(1)} %get-tuple-element.24.cols, ...), custom_call_target="tpu_custom_call" | custom-call | tf_op jit(solution)/shard_map/running_means/pallas_call | solution.py:234
  (4 shorter events, 0.1 us)

commit v5 on v4

--- a/solution.py
+++ b/solution.py
@@ -15,10 +15,12 @@
 LANES = 128
 T = 256
 NT = S // T
+NH = NT // 2
 SIB = 8
 RING = 8
 MSG = 136
-LHS = 208
+LHS = 144
+HALF = 1024
 
 
 ROOM = pltpu.CompilerParams(vmem_limit_bytes=16 << 20)
@@ -55,41 +57,58 @@
     return jnp.where(mask, 1.0, 0.0).astype(BF16)
 
 
-def sums_kernel(vt_far, gid_far, table_far, out, slot_out, local, cols, vt, gid, table, sems):
-    values_in = pltpu.make_async_copy(vt_far, vt, sems.at[0])
+def sums_kernel(vt_far, gid_far, table_far, out, slot_out, local, cols, vt, gid, table, split, sems):
+    values_in = [
+        pltpu.make_async_copy(vt_far.at[16 * g : 16 * g + 16], vt.at[16 * g : 16 * g + 16], sems.at[3 + g]) for g in range(4)
+    ]
     keys_in = pltpu.make_async_copy(gid_far, gid, sems.at[1])
     table_in = pltpu.make_async_copy(table_far, table, sems.at[2])
     keys_in.start()
     table_in.start()
-    values_in.start()
+    for copy in values_in:
+        copy.start()
     keys_in.wait()
     table_in.wait()
     slot = lookup(table[...], gid[...])
     slot_out[...] = slot
+    sub = lax.broadcasted_iota(jnp.int32, (16, LANES), 0)
+    ones = jnp.where(sub == 0, 1.0, 0.0)
+    spans = [slice(i * LANES, (i + 1) * LANES) for i in range(R // LANES)]
+    highs = [jnp.broadcast_to(slot[i : i + 1, :], (16, LANES)) >= HALF for i in range(R // LANES)]
+
+    def place(rows, value):
+        for at, high in zip(spans, highs):
+            v = value[:, at] if value.shape[1] > LANES else value
+            local[rows : rows + 16, at] = v.astype(BF16)
+            split[rows : rows + 16, at] = jnp.where(high, 0.0, v).astype(BF16)
+            split[LHS + rows : LHS + rows + 16, at] = jnp.where(high, v, 0.0).astype(BF16)
+
+    place(128, ones)
+    for g in range(4):
+        values_in[g].wait()
+        a, b, _ = pieces(vt[16 * g : 16 * g + 16, :])
+        place(16 * g, a.astype(F32))
+        place(64 + 16 * g, b.astype(F32))
     for i, block in enumerate(columns(slot)):
         cols[i * LANES : (i + 1) * LANES, :] = block
-    values_in.wait()
-    a, b, c = pieces(vt[...])
-    local[0:64, :] = a
-    local[64:128, :] = b
-    local[128:192, :] = c
-    sub = lax.broadcasted_iota(jnp.int32, (16, R), 0)
-    local[192:208, :] = jnp.where(sub == 0, 1.0, 0.0).astype(BF16)
     lane = lax.broadcasted_iota(jnp.int32, (T, T), 1)
     first = lax.broadcasted_iota(jnp.int32, (8, LANES), 0) == 0
-    for j in range(NT):
+    for j in range(NH):
         res = None
         for k in range(NT):
             at = slice(k * T, (k + 1) * T)
-            keys = cols[at, :]
+            keys = jnp.bitwise_and(cols[at, :], HALF - 1)
             keys = jnp.concatenate([keys, keys], axis=1)
-            part = dot(local[:, at], hot(keys == lane + j * T))
+            part = dot(split[:, at], hot(keys == lane + j * T))
             res = part if res is None else res + part
-        total = res[0:64] + (res[64:128] + res[128:192])
-        out[j, 0:64, :] = total[:, :LANES]
-        out[j, 64:128, :] = total[:, LANES:]
-        number = jnp.broadcast_to(res[192:193], (8, T))
-        out[j, 128:136, :] = jnp.where(first, number[:, :LANES], number[:, LANES:])
+        for h in range(2):
+            of = res[h * LHS : (h + 1) * LHS]
+            total = of[0:64] + of[64:128]
+            to = h * NH + j
+            out[to, 0:64, :] = total[:, :LANES]
+            out[to, 64:128, :] = total[:, LANES:]
+            number = jnp.broadcast_to(of[128:129], (8, T))
+            out[to, 128:136, :] = jnp.where(first, number[:, :LANES], number[:, LANES:])
 
 
 def slice_kernel(arrived, out):
@@ -146,37 +165,37 @@
     sub = lax.broadcasted_iota(jnp.int32, (16, LANES), 0)
     for j in range(NT):
         for h in range(2):
-            at = slice(j * T + h * LANES, j * T + (h + 1) * LANES)
-            a, b, c = pieces(start[j, h * 64 : (h + 1) * 64, :])
-            left[0:64, at] = a
-            left[64:128, at] = b
-            left[128:192, at] = c
-            a, b, c = (
-                jnp.broadcast_to(v.astype(F32), (16, LANES))
-                for v in pieces(start[j, 128 + h : 129 + h, :])
-            )
-            left[192:208, at] = jnp.where(
-                sub == 0, a, jnp.where(sub == 1, b, jnp.where(sub == 2, c, 0.0))
-            ).astype(BF16)
+            a, b, _ = pieces(start[j, h * 64 : (h + 1) * 64, :])
+            n = pieces(start[j, 128 + h : 129 + h, :])
+            n = [jnp.broadcast_to(v.astype(F32), (16, LANES)) for v in n]
+            n = jnp.where(sub == 0, n[0], jnp.where(sub == 1, n[1], jnp.where(sub == 2, n[2], 0.0)))
+            top = (j // NH) * LHS
+            at = (j % NH) * T + h * LANES
+            left[top : top + LHS, at : at + LANES] = jnp.concatenate([a, b, n.astype(BF16)], axis=0)
     label = lax.broadcasted_iota(jnp.int32, (T, T), 0)
     order = label <= lax.broadcasted_iota(jnp.int32, (T, T), 1)
     copies = []
     for j in range(NT):
         row = jnp.concatenate([slot[2 * j : 2 * j + 1, :], slot[2 * j + 1 : 2 * j + 2, :]], axis=1)
+        high = jnp.broadcast_to(row, (LHS, T)) >= HALF
         row = jnp.broadcast_to(row, (T, T))
+        low = jnp.bitwise_and(row, HALF - 1)
         res = None
-        for k in range(NT):
-            part = dot(left[:, k * T : (k + 1) * T], hot(label + k * T == row))
+        for k in range(NH):
+            part = dot(left[:, k * T : (k + 1) * T], hot(label + k * T == low))
             res = part if res is None else res + part
+        own = None
         for k in range(j + 1):
             at = slice(k * T, (k + 1) * T)
             keys = cols[at, :]
             mask = jnp.concatenate([keys, keys], axis=1) == row
             if k == j:
                 mask = jnp.logical_and(mask, order)
-            res = res + dot(local[:, at], hot(mask))
-        total = res[0:64] + (res[64:128] + res[128:192])
-        tally = (res[192:193] + res[193:194]) + res[194:195]
+            part = dot(local[:, at], hot(mask))
+            own = part if own is None else own + part
+        res = jnp.where(high, res[LHS : 2 * LHS], res[0:LHS]) + own
+        total = res[0:64] + res[64:128]
+        tally = (res[128:129] + res[129:130]) + res[130:131]
         at = slice(j * T, (j + 1) * T)
         held_mean[:, at] = total / tally
         copies.append(pltpu.make_async_copy(held_mean.at[:, at], mean.at[:, at], sems.at[j]))
@@ -222,7 +241,8 @@
             pltpu.VMEM((M, R), F32),
             pltpu.VMEM((16, LANES), jnp.int32),
             pltpu.VMEM((16, LANES), jnp.int32),
-            pltpu.SemaphoreType.DMA((3,)),
+            pltpu.VMEM((2 * LHS, R), BF16),
+            pltpu.SemaphoreType.DMA((7,)),
         ],
         compiler_params=ROOM,
         name="local_sums",
@@ -236,7 +256,7 @@
         out_shape=(shape(M, R), shape(16, LANES, dtype=jnp.int32), shape(M, 512)),
         out_specs=(pl.BlockSpec(memory_space=pl.ANY), vmem, vmem),
         scratch_shapes=[
-            pltpu.VMEM((LHS, S), BF16),
+            pltpu.VMEM((2 * LHS, HALF), BF16),
             pltpu.VMEM((M, R), F32),
             pltpu.SemaphoreType.DMA((NT,)),
         ],

time: 85.5 us -> 84.1 us (0.984)
  Pallas kernels: 7.91 us -> 6.5 us
    pallas_call x1, Pallas kernels: 4.52 us -> 3.6 us  [running_call(): pl.pallas_call(running_kernel, out_shape=(shape(M, R), shape(16, LANES, d...]
where the time goes in v5:
time: 84.1 us; the launch traced here: 83.8 us
  blocking collectives  76.6 us (91%)
  Pallas kernels  6.5 us (8%)
    all_to_all x1, blocking collectives, local(): arrived = held(lax.all_to_all(sums, siblings, 0, 0, tiled=True))  19.4 us
    all_to_all x1, blocking collectives, local(): along_y = held(lax.all_to_all(ring, 'y', 0, 0, tiled=True))  14.2 us
    all_to_all x1, blocking collectives, local(): along_z = held(lax.all_to_all(parts, 'z', 0, 0, tiled=True))  13.7 us
    all_to_all x1, blocking collectives, local(): start = held(lax.all_to_all(starts, siblings, 0, 0, tiled=True))  12.9 us
    all_to_all x1, blocking collectives, local(): back = held(lax.all_to_all(scanned, 'z', 0, 0, tiled=True))  10.3 us
    all_gather x1, blocking collectives, local(): closed = lax.all_gather(closing_half, 'c')  6.25 us
    pallas_call x1, Pallas kernels, running_call(): pl.pallas_call(running_kernel, out_shape=(shape(M, R), shape(16, LANES, d...  3.6 us
    pallas_call x1, Pallas kernels, sums_call(): pl.pallas_call(sums_kernel, in_specs=[outside] * 3, out_shape=(near(SIB,...  2.78 us

profile of v5, /device:TPU:1, one launch (start us, length us, event | category | flops | bytes accessed | tf_op | source)
XLA Modules:
  0.0 83.8 jit_solution(10036080274187703908)
XLA Ops:
  0.6 2.8 %local_sums.1 = (f32[8,136,128]{2,1,0:T(8,128)S(1)}, s32[16,128]{1,0:T(8,128)S(1)}, bf16[144,2048]{1,0:T(8,128)(2,1)S(1)}, s32[2048,128]{1,0:T(8,128)S(1)}) custom-call(f32[64,2048]{1,0:T(8,128)} %bitcast.8, s32[16,128]{1,0:T(8,128)} %bitcast.9, s32[16,128]{1,0:T(8,128)} %bitcast.10), custom_call_target="tpu_custom_call" | custom-call | tf_op jit(solution)/shard_map/local_sums/pallas_call | solution.py:231
  3.4 19.4 %all_to_all.25.arrived = f32[8,136,128]{2,1,0:T(8,128)S(1)} all-to-all(f32[8,136,128]{2,1,0:T(8,128)S(1)} %get-tuple-element.16), channel_id=1, replica_groups=mesh['y'=8,'z'=8,'c'=2,'x'=4] {'x','c'}, dimensions={0} | all-to-all | bytes 1114112 | tf_op jit(solution)/shard_map/all_to_all | solution.py:274
  22.8 13.7 %all_to_all.26.arrived = f32[8,24,128]{2,1,0:T(8,128)S(1)} all-to-all(f32[8,24,128]{2,1,0:T(8,128)S(1)} %slice_sums.1), channel_id=1, replica_groups=mesh['y'=8,'z'=8,'c'=2,'x'=4] {'z'}, dimensions={0} | all-to-all | bytes 196608 | tf_op jit(solution)/shard_map/all_to_all | solution.py:281
  36.5 14.2 %all_to_all.27.rings = f32[8,24,128]{2,1,0:T(8,128)S(1)} all-to-all(f32[8,24,128]{2,1,0:T(8,128)S(1)} %ring_sums.1), channel_id=1, replica_groups=mesh['y'=8,'z'=8,'c'=2,'x'=4] {'y'}, dimensions={0} | all-to-all | bytes 196608 | tf_op jit(solution)/shard_map/all_to_all | solution.py:288
  50.7 10.3 %all_to_all.28.far = f32[8,32,128]{2,1,0:T(8,128)S(1)} all-to-all(f32[8,32,128]{2,1,0:T(8,128)S(1)} %get-tuple-element.17), channel_id=1, replica_groups=mesh['y'=8,'z'=8,'c'=2,'x'=4] {'z'}, dimensions={0} | all-to-all | bytes 262144 | tf_op jit(solution)/shard_map/all_to_all | solution.py:295
  61.1 6.3 %all-gather = f32[256,128]{1,0:T(8,128)S(1)} all-gather(f32[128,128]{1,0:T(8,128)S(1)} %get-tuple-element.20), channel_id=2, replica_groups=mesh['y'=8,'z'=8,'c'=2,'x'=4] {'c'}, dimensions={0}, use_global_device_ids=true | all-gather | bytes 196608 | tf_op jit(solution)/shard_map/all_gather | solution.py:302
  67.3 12.9 %all_to_all.29.start = f32[8,136,128]{2,1,0:T(8,128)S(1)} all-to-all(f32[8,136,128]{2,1,0:T(8,128)S(1)} %get-tuple-element.21), channel_id=1, replica_groups=mesh['y'=8,'z'=8,'c'=2,'x'=4] {'x','c'}, dimensions={0} | all-to-all | bytes 1114112 | tf_op jit(solution)/shard_map/all_to_all | solution.py:305
  80.2 3.6 %running_means.1 = (f32[64,2048]{1,0:T(8,128)}, s32[16,128]{1,0:T(8,128)}, f32[64,512]{1,0:T(8,128)}) custom-call(f32[8,136,128]{2,1,0:T(8,128)S(1)} %all_to_all.29.start, bf16[144,2048]{1,0:T(8,128)(2,1)S(1)} %get-tuple-element.22.local, s32[16,128]{1,0:T(8,128)S(1)} %get-tuple-element.23.slot, s32[2048,128]{1,0:T(8,128)S(1)} %get-tuple-element.24.cols, ...), custom_call_target="tpu_custom_call" | custom-call | tf_op jit(solution)/shard_map/running_means/pallas_call | solution.py:254
  (4 shorter events, 0.1 us)

commit v6 on v5

--- a/solution.py
+++ b/solution.py
@@ -161,7 +161,30 @@
         acc = acc + arrived[i]
 
 
-def running_kernel(start, local, slot, cols, closed, mean, count, closing, left, held_mean, sems):
+def both(slot, j):
+    return jnp.concatenate([slot[2 * j : 2 * j + 1, :], slot[2 * j + 1 : 2 * j + 2, :]], axis=1)
+
+
+def own_kernel(local, slot, cols, out):
+    label = lax.broadcasted_iota(jnp.int32, (T, T), 0)
+    order = label <= lax.broadcasted_iota(jnp.int32, (T, T), 1)
+    for j in range(NT):
+        row = jnp.broadcast_to(both(slot, j), (T, T))
+        own = None
+        for k in range(j + 1):
+            at = slice(k * T, (k + 1) * T)
+            keys = cols[at, :]
+            mask = jnp.concatenate([keys, keys], axis=1) == row
+            if k == j:
+                mask = jnp.logical_and(mask, order)
+            part = dot(local[:, at], hot(mask))
+            own = part if own is None else own + part
+        at = slice(j * T, (j + 1) * T)
+        out[0:64, at] = own[0:64] + own[64:128]
+        out[64:72, at] = own[128:136]
+
+
+def running_kernel(start, own, slot, closed, mean, count, closing, left, held_mean, sems):
     sub = lax.broadcasted_iota(jnp.int32, (16, LANES), 0)
     for j in range(NT):
         for h in range(2):
@@ -173,30 +196,19 @@
             at = (j % NH) * T + h * LANES
             left[top : top + LHS, at : at + LANES] = jnp.concatenate([a, b, n.astype(BF16)], axis=0)
     label = lax.broadcasted_iota(jnp.int32, (T, T), 0)
-    order = label <= lax.broadcasted_iota(jnp.int32, (T, T), 1)
     copies = []
     for j in range(NT):
-        row = jnp.concatenate([slot[2 * j : 2 * j + 1, :], slot[2 * j + 1 : 2 * j + 2, :]], axis=1)
+        row = both(slot, j)
         high = jnp.broadcast_to(row, (LHS, T)) >= HALF
-        row = jnp.broadcast_to(row, (T, T))
-        low = jnp.bitwise_and(row, HALF - 1)
+        low = jnp.bitwise_and(jnp.broadcast_to(row, (T, T)), HALF - 1)
         res = None
         for k in range(NH):
             part = dot(left[:, k * T : (k + 1) * T], hot(label + k * T == low))
             res = part if res is None else res + part
-        own = None
-        for k in range(j + 1):
-            at = slice(k * T, (k + 1) * T)
-            keys = cols[at, :]
-            mask = jnp.concatenate([keys, keys], axis=1) == row
-            if k == j:
-                mask = jnp.logical_and(mask, order)
-            part = dot(local[:, at], hot(mask))
-            own = part if own is None else own + part
-        res = jnp.where(high, res[LHS : 2 * LHS], res[0:LHS]) + own
-        total = res[0:64] + res[64:128]
-        tally = (res[128:129] + res[129:130]) + res[130:131]
+        res = jnp.where(high, res[LHS : 2 * LHS], res[0:LHS])
         at = slice(j * T, (j + 1) * T)
+        total = res[0:64] + res[64:128] + own[0:64, at]
+        tally = (res[128:129] + res[129:130]) + res[130:131] + own[64:65, at]
         held_mean[:, at] = total / tally
         copies.append(pltpu.make_async_copy(held_mean.at[:, at], mean.at[:, at], sems.at[j]))
         copies[-1].start()
@@ -249,7 +261,17 @@
     )(outer(vt), outer(gid), outer(table))
 
 
-def running_call(start, local, slot, cols, closed):
+def own_call(local, slot, cols):
+    return pl.pallas_call(
+        own_kernel,
+        out_shape=near(72, R),
+        compiler_params=ROOM,
+        cost_estimate=pl.CostEstimate(flops=2 * 144 * R * R // 2, bytes_accessed=1 << 20, transcendentals=0),
+        name="own_rows",
+    )(held(local), held(slot), held(cols))
+
+
+def running_call(start, own, slot, closed):
     vmem = pl.BlockSpec(memory_space=pltpu.VMEM)
     return pl.pallas_call(
         running_kernel,
@@ -262,7 +284,7 @@
         ],
         compiler_params=ROOM,
         name="running_means",
-    )(start, held(local), held(slot), held(cols), closed)
+    )(start, held(own), held(slot), closed)
 
 
 def local(values, group_ids, slot_of):
@@ -299,11 +321,10 @@
         compiler_params=ROOM,
         name="starts",
     )(back, arrived, counts)
-    closed = lax.all_gather(closing_half, "c")
-    starts, closed = lax.optimization_barrier((starts, closed))
-    closed = held(closed)
+    closed = held(lax.all_gather(closing_half, "c"))
+    own = own_call(local_pieces, slot, cols)
     start = held(lax.all_to_all(starts, siblings, 0, 0, tiled=True))
-    mean, count, closing = running_call(start, local_pieces, slot, cols, closed)
+    mean, count, closing = running_call(start, own, slot, closed)
     return mean.T, count.reshape(R), closing.T
 
 

time: 84.1 us -> 83 us (0.987)
  blocking collectives: 76.6 us -> 59.4 us
  starting transfers between devices: 0 us -> 8.14 us
  waiting for transfers between devices: 0 us -> 6.96 us
  Pallas kernels: 6.5 us -> 7.43 us
    all_to_all x1 -> x0, blocking collectives: 12.9 us -> none  [local(): start = held(lax.all_to_all(starts, siblings, 0, 0, tiled=True))]
    all_to_all x0 -> x1, starting transfers between devices: none -> 8.14 us  [local(): start = held(lax.all_to_all(starts, siblings, 0, 0, tiled=True))]
    all_to_all x0 -> x1, waiting for transfers between devices: none -> 6.96 us  [local(): start = held(lax.all_to_all(starts, siblings, 0, 0, tiled=True))]
    all_gather x1, blocking collectives: 6.25 us -> 1.9 us  [local(): closed = held(lax.all_gather(closing_half, 'c'))]
    pallas_call x0 -> x1, Pallas kernels: none -> 0.86 us  [own_call(): pl.pallas_call(own_kernel, out_shape=near(72, R), compiler_params=ROOM, c...]
  transfers between devices with their start and end apart: 0 -> 1, of which waited for: 0 -> 1; matrix products, arithmetic and copies ran while one was open for 0% -> 0% of each run, Pallas kernels for 0% -> 1%
where the time goes in v6:
time: 83 us; the launch traced here: 82.6 us
  blocking collectives  59.4 us (72%)
  starting transfers between devices  8.14 us (10%)
  Pallas kernels  7.43 us (9%)
  waiting for transfers between devices  6.96 us (8%)
    all_to_all x1, blocking collectives, local(): arrived = held(lax.all_to_all(sums, siblings, 0, 0, tiled=True))  19.4 us
    all_to_all x1, blocking collectives, local(): along_y = held(lax.all_to_all(ring, 'y', 0, 0, tiled=True))  14.2 us
    all_to_all x1, blocking collectives, local(): along_z = held(lax.all_to_all(parts, 'z', 0, 0, tiled=True))  13.7 us
    all_to_all x1, blocking collectives, local(): back = held(lax.all_to_all(scanned, 'z', 0, 0, tiled=True))  10.3 us
    all_to_all x1, starting transfers between devices, local(): start = held(lax.all_to_all(starts, siblings, 0, 0, tiled=True))  8.14 us
    all_to_all x1, waiting for transfers between devices, local(): start = held(lax.all_to_all(starts, siblings, 0, 0, tiled=True))  6.96 us
    pallas_call x1, Pallas kernels, running_call(): pl.pallas_call(running_kernel, out_shape=(shape(M, R), shape(16, LANES, d...  2.88 us
    pallas_call x1, Pallas kernels, sums_call(): pl.pallas_call(sums_kernel, in_specs=[outside] * 3, out_shape=(near(SIB,...  2.77 us
  transfers between devices with their start and end apart: 1, of which 1 were waited for; matrix products, arithmetic and copies ran while one was open for 0% of the time, Pallas kernels for 1%

profile of v6, /device:TPU:1, one launch (start us, length us, event | category | flops | bytes accessed | tf_op | source)
XLA Modules:
  0.0 82.6 jit_solution(7733139606351177096)
XLA Ops:
  0.6 2.8 %local_sums.1 = (f32[8,136,128]{2,1,0:T(8,128)S(1)}, s32[16,128]{1,0:T(8,128)S(1)}, bf16[144,2048]{1,0:T(8,128)(2,1)S(1)}, s32[2048,128]{1,0:T(8,128)S(1)}) custom-call(f32[64,2048]{1,0:T(8,128)} %bitcast.8, s32[16,128]{1,0:T(8,128)} %bitcast.9, s32[16,128]{1,0:T(8,128)} %bitcast.10), custom_call_target="tpu_custom_call" | custom-call | tf_op jit(solution)/shard_map/local_sums/pallas_call | solution.py:243
  3.4 19.4 %all_to_all.25.arrived = f32[8,136,128]{2,1,0:T(8,128)S(1)} all-to-all(f32[8,136,128]{2,1,0:T(8,128)S(1)} %get-tuple-element.14), channel_id=1, replica_groups=mesh['y'=8,'z'=8,'c'=2,'x'=4] {'x','c'}, dimensions={0} | all-to-all | bytes 1114112 | tf_op jit(solution)/shard_map/all_to_all | solution.py:296
  22.8 13.7 %all_to_all.26.arrived = f32[8,24,128]{2,1,0:T(8,128)S(1)} all-to-all(f32[8,24,128]{2,1,0:T(8,128)S(1)} %slice_sums.1), channel_id=1, replica_groups=mesh['y'=8,'z'=8,'c'=2,'x'=4] {'z'}, dimensions={0} | all-to-all | bytes 196608 | tf_op jit(solution)/shard_map/all_to_all | solution.py:303
  36.5 14.2 %all_to_all.27.rings = f32[8,24,128]{2,1,0:T(8,128)S(1)} all-to-all(f32[8,24,128]{2,1,0:T(8,128)S(1)} %ring_sums.1), channel_id=1, replica_groups=mesh['y'=8,'z'=8,'c'=2,'x'=4] {'y'}, dimensions={0} | all-to-all | bytes 196608 | tf_op jit(solution)/shard_map/all_to_all | solution.py:310
  50.7 10.3 %all_to_all.28.far = f32[8,32,128]{2,1,0:T(8,128)S(1)} all-to-all(f32[8,32,128]{2,1,0:T(8,128)S(1)} %get-tuple-element.15), channel_id=1, replica_groups=mesh['y'=8,'z'=8,'c'=2,'x'=4] {'z'}, dimensions={0} | all-to-all | bytes 262144 | tf_op jit(solution)/shard_map/all_to_all | solution.py:317
  61.0 0.8 %starts.1 = (f32[8,136,128]{2,1,0:T(8,128)}, f32[128,128]{1,0:T(8,128)S(1)}) custom-call(f32[8,32,128]{2,1,0:T(8,128)S(1)} %all_to_all.28.far, f32[8,136,128]{2,1,0:T(8,128)S(1)} %all_to_all.25.arrived, f32[8,128]{1,0:T(8,128)S(1)} %get-tuple-element.16.counts), custom_call_target="tpu_custom_call" | custom-call | tf_op jit(solution)/shard_map/starts/pallas_call | solution.py:318
  61.9 8.1 %all-to-all-start.4 = ((f32[8,136,128]{2,1,0:T(8,128)}), f32[8,136,128]{2,1,0:T(8,128)S(1)}, u32[]{:S(2)}, u32[]{:S(2)}) async-start(f32[8,136,128]{2,1,0:T(8,128)} %get-tuple-element.17), calls=%async_computation.4 | async-start | bytes 1114112 | tf_op jit(solution)/shard_map/all_to_all | solution.py:326
  70.0 0.9 %own_rows.1.own = f32[72,2048]{1,0:T(8,128)S(1)} custom-call(bf16[144,2048]{1,0:T(8,128)(2,1)S(1)} %get-tuple-element.18.local, s32[16,128]{1,0:T(8,128)S(1)} %get-tuple-element.19.slot, s32[2048,128]{1,0:T(8,128)S(1)} %get-tuple-element.20.cols), custom_call_target="tpu_custom_call" | custom-call | flops 603979776 | bytes 1048576 | tf_op jit(solution)/shard_map/own_rows/pallas_call | solution.py:265
  70.9 1.9 %all-gather = f32[256,128]{1,0:T(8,128)S(1)} all-gather(f32[128,128]{1,0:T(8,128)S(1)} %get-tuple-element.21), channel_id=2, replica_groups=mesh['y'=8,'z'=8,'c'=2,'x'=4] {'c'}, dimensions={0}, use_global_device_ids=true | all-gather | bytes 196608 | tf_op jit(solution)/shard_map/all_gather | solution.py:324
  72.8 7.0 %all-to-all-done.4.start = f32[8,136,128]{2,1,0:T(8,128)S(1)} async-done(((f32[8,136,128]{2,1,0:T(8,128)}), f32[8,136,128]{2,1,0:T(8,128)S(1)}, u32[]{:S(2)}, u32[]{:S(2)}) %all-to-all-start.4) | async-done | bytes 557088 | tf_op jit(solution)/shard_map/all_to_all | solution.py:326
  79.7 2.9 %running_means.1 = (f32[64,2048]{1,0:T(8,128)}, s32[16,128]{1,0:T(8,128)}, f32[64,512]{1,0:T(8,128)}) custom-call(f32[8,136,128]{2,1,0:T(8,128)S(1)} %all-to-all-done.4.start, f32[72,2048]{1,0:T(8,128)S(1)} %own_rows.1.own, s32[16,128]{1,0:T(8,128)S(1)} %get-tuple-element.19.slot, f32[2,128,128]{2,1,0:T(8,128)S(1)} %bitcast.7), custom_call_target="tpu_custom_call" | custom-call | tf_op jit(solution)/shard_map/running_means/pallas_call | solution.py:276
  (3 shorter events, 0.1 us)
Async XLA Ops:
  61.9 17.9 %all-to-all-start.4 = ((f32[8,136,128]{2,1,0:T(8,128)}), f32[8,136,128]{2,1,0:T(8,128)S(1)}, u32[]{:S(2)}, u32[]{:S(2)}) async-start(f32[8,136,128]{2,1,0:T(8,128)} %get-tuple-element.17), calls=%async_computation.4 | async-start | bytes 1114112 | tf_op jit(solution)/shard_map/all_to_all | solution.py:326

commit v7 on v6

--- a/solution.py
+++ b/solution.py
@@ -57,7 +57,7 @@
     return jnp.where(mask, 1.0, 0.0).astype(BF16)
 
 
-def sums_kernel(vt_far, gid_far, table_far, out, slot_out, local, cols, vt, gid, table, split, sems):
+def sums_kernel(vt_far, gid_far, table_far, out, slot_out, split, cols, vt, gid, table, sems):
     values_in = [
         pltpu.make_async_copy(vt_far.at[16 * g : 16 * g + 16], vt.at[16 * g : 16 * g + 16], sems.at[3 + g]) for g in range(4)
     ]
@@ -72,23 +72,24 @@
     slot = lookup(table[...], gid[...])
     slot_out[...] = slot
     sub = lax.broadcasted_iota(jnp.int32, (16, LANES), 0)
-    ones = jnp.where(sub == 0, 1.0, 0.0)
+    ones = jnp.where(sub == 0, 1.0, 0.0).astype(BF16)
     spans = [slice(i * LANES, (i + 1) * LANES) for i in range(R // LANES)]
-    highs = [jnp.broadcast_to(slot[i : i + 1, :], (16, LANES)) >= HALF for i in range(R // LANES)]
-
-    def place(rows, value):
-        for at, high in zip(spans, highs):
-            v = value[:, at] if value.shape[1] > LANES else value
-            local[rows : rows + 16, at] = v.astype(BF16)
-            split[rows : rows + 16, at] = jnp.where(high, 0.0, v).astype(BF16)
-            split[LHS + rows : LHS + rows + 16, at] = jnp.where(high, v, 0.0).astype(BF16)
-
-    place(128, ones)
+    high = jnp.where(slot >= HALF, 1.0, 0.0)
+    highs = [jnp.broadcast_to(high[i : i + 1, :], (16, LANES)) for i in range(R // LANES)]
+    picks = [((1.0 - h).astype(BF16), h.astype(BF16)) for h in highs]
+
+    def place(rows, at, value, pick):
+        split[rows : rows + 16, at] = value * pick[0]
+        split[LHS + rows : LHS + rows + 16, at] = value * pick[1]
+
+    for at, pick in zip(spans, picks):
+        place(128, at, ones, pick)
     for g in range(4):
         values_in[g].wait()
-        a, b, _ = pieces(vt[16 * g : 16 * g + 16, :])
-        place(16 * g, a.astype(F32))
-        place(64 + 16 * g, b.astype(F32))
+        for at, pick in zip(spans, picks):
+            a, b, _ = pieces(vt[16 * g : 16 * g + 16, at])
+            place(16 * g, at, a, pick)
+            place(64 + 16 * g, at, b, pick)
     for i, block in enumerate(columns(slot)):
         cols[i * LANES : (i + 1) * LANES, :] = block
     lane = lax.broadcasted_iota(jnp.int32, (T, T), 1)
@@ -149,23 +150,29 @@
     counts_out[...] = counts
 
 
-def start_kernel(far, arrived, counts, out, closing):
+def start_kernel(far, arrived, counts, out_far, closing, out, sems):
     parts = []
     for p in range(RING):
         parts.append(far[p, 0:16, :])
         closing[16 * p : 16 * p + 16, :] = far[p, 16:32, :]
     acc = jnp.concatenate(parts + [counts[...]], axis=0)
+    copies = []
     for k in range(SIB):
         i = 2 * (k % 4) + k // 4
         out[i] = acc
+        copies.append(pltpu.make_async_copy(out.at[i], out_far.at[i], sems.at[i]))
+        copies[-1].start()
         acc = acc + arrived[i]
+    for copy in copies:
+        copy.wait()
 
 
 def both(slot, j):
     return jnp.concatenate([slot[2 * j : 2 * j + 1, :], slot[2 * j + 1 : 2 * j + 2, :]], axis=1)
 
 
-def own_kernel(local, slot, cols, out):
+def own_kernel(split, slot, cols, out, local):
+    local[...] = split[0:LHS, :] + split[LHS : 2 * LHS, :]
     label = lax.broadcasted_iota(jnp.int32, (T, T), 0)
     order = label <= lax.broadcasted_iota(jnp.int32, (T, T), 1)
     for j in range(NT):
@@ -184,7 +191,12 @@
         out[64:72, at] = own[128:136]
 
 
-def running_kernel(start, own, slot, closed, mean, count, closing, left, held_mean, sems):
+def running_kernel(start, own, slot, closed, mean, count_far, closing_far, left, held_mean, count, closing, sems):
+    for c in range(2):
+        for h in range(2):
+            closing[:, c * T + h * LANES : c * T + (h + 1) * LANES] = closed[c, h * 64 : (h + 1) * 64, :]
+    copies = [pltpu.make_async_copy(closing, closing_far, sems.at[NT])]
+    copies[0].start()
     sub = lax.broadcasted_iota(jnp.int32, (16, LANES), 0)
     for j in range(NT):
         for h in range(2):
@@ -196,7 +208,6 @@
             at = (j % NH) * T + h * LANES
             left[top : top + LHS, at : at + LANES] = jnp.concatenate([a, b, n.astype(BF16)], axis=0)
     label = lax.broadcasted_iota(jnp.int32, (T, T), 0)
-    copies = []
     for j in range(NT):
         row = both(slot, j)
         high = jnp.broadcast_to(row, (LHS, T)) >= HALF
@@ -215,9 +226,8 @@
         whole = tally.astype(jnp.int32)
         count[2 * j : 2 * j + 1, :] = whole[:, :LANES]
         count[2 * j + 1 : 2 * j + 2, :] = whole[:, LANES:]
-    for c in range(2):
-        for h in range(2):
-            closing[:, c * T + h * LANES : c * T + (h + 1) * LANES] = closed[c, h * 64 : (h + 1) * 64, :]
+    copies.append(pltpu.make_async_copy(count, count_far, sems.at[NT + 1]))
+    copies[-1].start()
     for copy in copies:
         copy.wait()
 
@@ -228,6 +238,10 @@
 
 def near(*dims, dtype=F32):
     return pltpu.VMEM(dims, dtype)
+
+
+def outward(*dims):
+    return pltpu.HBM(dims, F32)
 
 
 def outer(x):
@@ -246,14 +260,13 @@
         out_shape=(
             near(SIB, MSG, LANES),
             near(16, LANES, dtype=jnp.int32),
-            near(LHS, R, dtype=BF16),
+            near(2 * LHS, R, dtype=BF16),
             near(R, LANES, dtype=jnp.int32),
         ),
         scratch_shapes=[
             pltpu.VMEM((M, R), F32),
             pltpu.VMEM((16, LANES), jnp.int32),
             pltpu.VMEM((16, LANES), jnp.int32),
-            pltpu.VMEM((2 * LHS, R), BF16),
             pltpu.SemaphoreType.DMA((7,)),
         ],
         compiler_params=ROOM,
@@ -261,26 +274,28 @@
     )(outer(vt), outer(gid), outer(table))
 
 
-def own_call(local, slot, cols):
+def own_call(split, slot, cols):
     return pl.pallas_call(
         own_kernel,
         out_shape=near(72, R),
+        scratch_shapes=[pltpu.VMEM((LHS, R), BF16)],
         compiler_params=ROOM,
         cost_estimate=pl.CostEstimate(flops=2 * 144 * R * R // 2, bytes_accessed=1 << 20, transcendentals=0),
         name="own_rows",
-    )(held(local), held(slot), held(cols))
+    )(held(split), held(slot), held(cols))
 
 
 def running_call(start, own, slot, closed):
-    vmem = pl.BlockSpec(memory_space=pltpu.VMEM)
     return pl.pallas_call(
         running_kernel,
         out_shape=(shape(M, R), shape(16, LANES, dtype=jnp.int32), shape(M, 512)),
-        out_specs=(pl.BlockSpec(memory_space=pl.ANY), vmem, vmem),
+        out_specs=(pl.BlockSpec(memory_space=pl.ANY),) * 3,
         scratch_shapes=[
             pltpu.VMEM((2 * LHS, HALF), BF16),
             pltpu.VMEM((M, R), F32),
-            pltpu.SemaphoreType.DMA((NT,)),
+            pltpu.VMEM((16, LANES), jnp.int32),
+            pltpu.VMEM((M, 2 * T), F32),
+            pltpu.SemaphoreType.DMA((NT + 2,)),
         ],
         compiler_params=ROOM,
         name="running_means",
@@ -291,7 +306,7 @@
     vt = values.T
     gid = group_ids.reshape(16, LANES)
     table = slot_of.reshape(16, LANES)
-    sums, slot, local_pieces, cols = sums_call(vt, gid, table)
+    sums, slot, split, cols = sums_call(vt, gid, table)
     siblings = ("x", "c")
     arrived = held(lax.all_to_all(sums, siblings, 0, 0, tiled=True))
     parts = pl.pallas_call(
@@ -317,12 +332,14 @@
     back = held(lax.all_to_all(scanned, "z", 0, 0, tiled=True))
     starts, closing_half = pl.pallas_call(
         start_kernel,
-        out_shape=(near(SIB, MSG, LANES), near(LANES, LANES)),
+        out_shape=(outward(SIB, MSG, LANES), near(LANES, LANES)),
+        out_specs=(pl.BlockSpec(memory_space=pl.ANY), pl.BlockSpec(memory_space=pltpu.VMEM)),
+        scratch_shapes=[pltpu.VMEM((SIB, MSG, LANES), F32), pltpu.SemaphoreType.DMA((SIB,))],
         compiler_params=ROOM,
         name="starts",
     )(back, arrived, counts)
     closed = held(lax.all_gather(closing_half, "c"))
-    own = own_call(local_pieces, slot, cols)
+    own = own_call(split, slot, cols)
     start = held(lax.all_to_all(starts, siblings, 0, 0, tiled=True))
     mean, count, closing = running_call(start, own, slot, closed)
     return mean.T, count.reshape(R), closing.T

time: 83 us -> 82.4 us (level)
  no operation moved by 1% of the time
where the time goes in v7:
time: 82.4 us; the launch traced here: 82 us
  blocking collectives  59.4 us (72%)
  starting transfers between devices  8.16 us (10%)
  waiting for transfers between devices  6.95 us (8%)
  Pallas kernels  6.85 us (8%)
    all_to_all x1, blocking collectives, local(): arrived = held(lax.all_to_all(sums, siblings, 0, 0, tiled=True))  19.4 us
    all_to_all x1, blocking collectives, local(): along_y = held(lax.all_to_all(ring, 'y', 0, 0, tiled=True))  14.2 us
    all_to_all x1, blocking collectives, local(): along_z = held(lax.all_to_all(parts, 'z', 0, 0, tiled=True))  13.7 us
    all_to_all x1, blocking collectives, local(): back = held(lax.all_to_all(scanned, 'z', 0, 0, tiled=True))  10.3 us
    all_to_all x1, starting transfers between devices, local(): start = held(lax.all_to_all(starts, siblings, 0, 0, tiled=True))  8.16 us
    all_to_all x1, waiting for transfers between devices, local(): start = held(lax.all_to_all(starts, siblings, 0, 0, tiled=True))  6.95 us
    pallas_call x1, Pallas kernels, sums_call(): pl.pallas_call(sums_kernel, in_specs=[outside] * 3, out_shape=(near(SIB,...  2.77 us
    pallas_call x1, Pallas kernels, running_call(): pl.pallas_call(running_kernel, out_shape=(shape(M, R), shape(16, LANES, d...  2.24 us
  transfers between devices with their start and end apart: 1, of which 1 were waited for; matrix products, arithmetic and copies ran while one was open for 0% of the time, Pallas kernels for 1%

profile of v7, /device:TPU:1, one launch (start us, length us, event | category | flops | bytes accessed | tf_op | source)
XLA Modules:
  0.0 82.0 jit_solution(1717677975399680263)
XLA Ops:
  0.6 2.8 %local_sums.1 = (f32[8,136,128]{2,1,0:T(8,128)S(1)}, s32[16,128]{1,0:T(8,128)S(1)}, bf16[288,2048]{1,0:T(8,128)(2,1)S(1)}, s32[2048,128]{1,0:T(8,128)S(1)}) custom-call(f32[64,2048]{1,0:T(8,128)} %bitcast.8, s32[16,128]{1,0:T(8,128)} %bitcast.9, s32[16,128]{1,0:T(8,128)} %bitcast.10), custom_call_target="tpu_custom_call" | custom-call | tf_op jit(solution)/shard_map/local_sums/pallas_call | solution.py:257
  3.4 19.4 %all_to_all.25.arrived = f32[8,136,128]{2,1,0:T(8,128)S(1)} all-to-all(f32[8,136,128]{2,1,0:T(8,128)S(1)} %get-tuple-element.14), channel_id=1, replica_groups=mesh['y'=8,'z'=8,'c'=2,'x'=4] {'x','c'}, dimensions={0} | all-to-all | bytes 1114112 | tf_op jit(solution)/shard_map/all_to_all | solution.py:311
  22.8 13.7 %all_to_all.26.arrived = f32[8,24,128]{2,1,0:T(8,128)S(1)} all-to-all(f32[8,24,128]{2,1,0:T(8,128)S(1)} %slice_sums.1), channel_id=1, replica_groups=mesh['y'=8,'z'=8,'c'=2,'x'=4] {'z'}, dimensions={0} | all-to-all | bytes 196608 | tf_op jit(solution)/shard_map/all_to_all | solution.py:318
  36.5 14.2 %all_to_all.27.rings = f32[8,24,128]{2,1,0:T(8,128)S(1)} all-to-all(f32[8,24,128]{2,1,0:T(8,128)S(1)} %ring_sums.1), channel_id=1, replica_groups=mesh['y'=8,'z'=8,'c'=2,'x'=4] {'y'}, dimensions={0} | all-to-all | bytes 196608 | tf_op jit(solution)/shard_map/all_to_all | solution.py:325
  50.7 10.3 %all_to_all.28.far = f32[8,32,128]{2,1,0:T(8,128)S(1)} all-to-all(f32[8,32,128]{2,1,0:T(8,128)S(1)} %get-tuple-element.15), channel_id=1, replica_groups=mesh['y'=8,'z'=8,'c'=2,'x'=4] {'z'}, dimensions={0} | all-to-all | bytes 262144 | tf_op jit(solution)/shard_map/all_to_all | solution.py:332
  61.0 0.9 %starts.1 = (f32[8,136,128]{2,1,0:T(8,128)}, f32[128,128]{1,0:T(8,128)S(1)}) custom-call(f32[8,32,128]{2,1,0:T(8,128)S(1)} %all_to_all.28.far, f32[8,136,128]{2,1,0:T(8,128)S(1)} %all_to_all.25.arrived, f32[8,128]{1,0:T(8,128)S(1)} %get-tuple-element.16.counts), custom_call_target="tpu_custom_call" | custom-call | tf_op jit(solution)/shard_map/starts/pallas_call | solution.py:333
  61.9 8.2 %all-to-all-start.4 = ((f32[8,136,128]{2,1,0:T(8,128)}), f32[8,136,128]{2,1,0:T(8,128)S(1)}, u32[]{:S(2)}, u32[]{:S(2)}) async-start(f32[8,136,128]{2,1,0:T(8,128)} %get-tuple-element.17), calls=%async_computation.4 | async-start | bytes 1114112 | tf_op jit(solution)/shard_map/all_to_all | solution.py:343
  70.1 0.9 %own_rows.1.own = f32[72,2048]{1,0:T(8,128)S(1)} custom-call(bf16[288,2048]{1,0:T(8,128)(2,1)S(1)} %get-tuple-element.18.split, s32[16,128]{1,0:T(8,128)S(1)} %get-tuple-element.19.slot, s32[2048,128]{1,0:T(8,128)S(1)} %get-tuple-element.20.cols), custom_call_target="tpu_custom_call" | custom-call | flops 603979776 | bytes 1048576 | tf_op jit(solution)/shard_map/own_rows/pallas_call | solution.py:278
  70.9 1.9 %all-gather = f32[256,128]{1,0:T(8,128)S(1)} all-gather(f32[128,128]{1,0:T(8,128)S(1)} %get-tuple-element.21), channel_id=2, replica_groups=mesh['y'=8,'z'=8,'c'=2,'x'=4] {'c'}, dimensions={0}, use_global_device_ids=true | all-gather | bytes 196608 | tf_op jit(solution)/shard_map/all_gather | solution.py:341
  72.8 6.9 %all-to-all-done.4.start = f32[8,136,128]{2,1,0:T(8,128)S(1)} async-done(((f32[8,136,128]{2,1,0:T(8,128)}), f32[8,136,128]{2,1,0:T(8,128)S(1)}, u32[]{:S(2)}, u32[]{:S(2)}) %all-to-all-start.4) | async-done | bytes 557088 | tf_op jit(solution)/shard_map/all_to_all | solution.py:343
  79.8 2.2 %running_means.1 = (f32[64,2048]{1,0:T(8,128)}, s32[16,128]{1,0:T(8,128)}, f32[64,512]{1,0:T(8,128)}) custom-call(f32[8,136,128]{2,1,0:T(8,128)S(1)} %all-to-all-done.4.start, f32[72,2048]{1,0:T(8,128)S(1)} %own_rows.1.own, s32[16,128]{1,0:T(8,128)S(1)} %get-tuple-element.19.slot, f32[2,128,128]{2,1,0:T(8,128)S(1)} %bitcast.7), custom_call_target="tpu_custom_call" | custom-call | tf_op jit(solution)/shard_map/running_means/pallas_call | solution.py:289
  (3 shorter events, 0.1 us)
Async XLA Ops:
  61.9 17.9 %all-to-all-start.4 = ((f32[8,136,128]{2,1,0:T(8,128)}), f32[8,136,128]{2,1,0:T(8,128)S(1)}, u32[]{:S(2)}, u32[]{:S(2)}) async-start(f32[8,136,128]{2,1,0:T(8,128)} %get-tuple-element.17), calls=%async_computation.4 | async-start | bytes 1114112 | tf_op jit(solution)/shard_map/all_to_all | solution.py:343

commit v8 on v7

--- a/solution.py
+++ b/solution.py
@@ -17,7 +17,7 @@
 NT = S // T
 NH = NT // 2
 SIB = 8
-RING = 8
+FAR = 64
 MSG = 136
 LHS = 144
 HALF = 1024
@@ -112,50 +112,40 @@
             out[to, 128:136, :] = jnp.where(first, number[:, :LANES], number[:, LANES:])
 
 
-def slice_kernel(arrived, out):
+def slice_kernel(arrived, out, buf):
     total = arrived[0]
     for i in range(1, SIB):
         total = total + arrived[i]
-    for p in range(RING):
-        out[p, 0:16, :] = total[16 * p : 16 * p + 16]
-        out[p, 16:24, :] = total[128:136]
-
-
-def ring_kernel(arrived, out):
-    total = arrived[0]
-    for i in range(1, RING):
-        total = total + arrived[i]
-    for p in range(RING):
-        out[p] = total
-
-
-def scan_kernel(arrived, rings, out, counts_out):
-    y = lax.axis_index("y")
-    z = lax.axis_index("z")
-    total = rings[0]
-    before = jnp.where(y > 0, total, 0.0)
-    for i in range(1, RING):
-        ring = rings[i]
-        before = before + jnp.where(i < y, ring, 0.0)
-        total = total + ring
-    number = jnp.where(z < RING // 2, total[16:17], total[17:18])
-    closing = total[0:16] / jnp.maximum(number, 1.0)
-    counts = before[16:24]
-    acc = before[0:16]
-    for p in range(RING):
-        out[p, 0:16, :] = acc
-        out[p, 16:32, :] = closing
-        acc = acc + arrived[p, 0:16, :]
-        counts = counts + jnp.where(p < z, arrived[p, 16:24, :], 0.0)
-    counts_out[...] = counts
-
-
-def start_kernel(far, arrived, counts, out_far, closing, out, sems):
-    parts = []
-    for p in range(RING):
-        parts.append(far[p, 0:16, :])
-        closing[16 * p : 16 * p + 16, :] = far[p, 16:32, :]
-    acc = jnp.concatenate(parts + [counts[...]], axis=0)
+    buf[...] = total
+    counts = buf[128:130, :]
+    for p in range(FAR):
+        out[p, 0:2, :] = buf[2 * p : 2 * p + 2, :]
+        out[p, 2:4, :] = counts
+
+
+def scan_kernel(arrived, out, counts_out):
+    mine = lax.axis_index("y") * 8 + lax.axis_index("z")
+    acc = jnp.zeros((4, LANES), F32)
+    before = jnp.zeros((4, LANES), F32)
+    for p in range(FAR):
+        got = arrived[p]
+        out[p, 0:2, :] = acc[0:2]
+        before = before + jnp.where(p < mine, got, 0.0)
+        acc = acc + got
+    number = jnp.where(mine < FAR // 2, acc[2:3], acc[3:4])
+    closing = acc[0:2] / jnp.maximum(number, 1.0)
+    for p in range(FAR):
+        out[p, 2:4, :] = closing
+    counts_out[0:2, :] = before[2:4]
+
+
+def start_kernel(far, arrived, counts, out_far, closing, out, buf, sems):
+    for p in range(FAR):
+        buf[2 * p : 2 * p + 2, :] = far[p, 0:2, :]
+        closing[2 * p : 2 * p + 2, :] = far[p, 2:4, :]
+    buf[128:130, :] = counts[0:2, :]
+    buf[130:136, :] = jnp.zeros((6, LANES), F32)
+    acc = buf[...]
     copies = []
     for k in range(SIB):
         i = 2 * (k % 4) + k // 4
@@ -309,32 +299,31 @@
     sums, slot, split, cols = sums_call(vt, gid, table)
     siblings = ("x", "c")
     arrived = held(lax.all_to_all(sums, siblings, 0, 0, tiled=True))
-    parts = pl.pallas_call(
+    far = ("y", "z")
+    pieces_out = pl.pallas_call(
         slice_kernel,
-        out_shape=near(RING, 24, LANES),
+        out_shape=near(FAR, 4, LANES),
+        scratch_shapes=[pltpu.VMEM((MSG, LANES), F32)],
         compiler_params=ROOM,
         name="slice_sums",
     )(arrived)
-    along_z = held(lax.all_to_all(parts, "z", 0, 0, tiled=True))
-    ring = pl.pallas_call(
-        ring_kernel,
-        out_shape=near(RING, 24, LANES),
-        compiler_params=ROOM,
-        name="ring_sums",
-    )(along_z)
-    along_y = held(lax.all_to_all(ring, "y", 0, 0, tiled=True))
+    met = held(lax.all_to_all(pieces_out, far, 0, 0, tiled=True))
     scanned, counts = pl.pallas_call(
         scan_kernel,
-        out_shape=(near(RING, 32, LANES), near(8, LANES)),
+        out_shape=(near(FAR, 4, LANES), near(8, LANES)),
         compiler_params=ROOM,
         name="scan",
-    )(along_z, along_y)
-    back = held(lax.all_to_all(scanned, "z", 0, 0, tiled=True))
+    )(met)
+    back = held(lax.all_to_all(scanned, far, 0, 0, tiled=True))
     starts, closing_half = pl.pallas_call(
         start_kernel,
         out_shape=(outward(SIB, MSG, LANES), near(LANES, LANES)),
         out_specs=(pl.BlockSpec(memory_space=pl.ANY), pl.BlockSpec(memory_space=pltpu.VMEM)),
-        scratch_shapes=[pltpu.VMEM((SIB, MSG, LANES), F32), pltpu.SemaphoreType.DMA((SIB,))],
+        scratch_shapes=[
+            pltpu.VMEM((SIB, MSG, LANES), F32),
+            pltpu.VMEM((MSG, LANES), F32),
+            pltpu.SemaphoreType.DMA((SIB,)),
+        ],
         compiler_params=ROOM,
         name="starts",
     )(back, arrived, counts)

time: 82.4 us -> 82.2 us (level)
  starting transfers between devices: 8.16 us -> 6.6 us
  blocking collectives: 59.4 us -> 60.7 us
    all_to_all x1, starting transfers between devices: 8.16 us -> 6.6 us  [local(): start = held(lax.all_to_all(starts, siblings, 0, 0, tiled=True))]
    all_to_all x3 -> x2, blocking collectives: 38.2 us -> 39.4 us  [the longest x1 24 us: local(): met = held(lax.all_to_all(pieces_out, far, 0, 0, tiled=True))]
where the time goes in v8:
time: 82.2 us; the launch traced here: 81.9 us
  blocking collectives  60.7 us (74%)
  Pallas kernels  6.98 us (8%)
  waiting for transfers between devices  6.94 us (8%)
  starting transfers between devices  6.6 us (8%)
    all_to_all x1, blocking collectives, local(): met = held(lax.all_to_all(pieces_out, far, 0, 0, tiled=True))  24 us
    all_to_all x1, blocking collectives, local(): arrived = held(lax.all_to_all(sums, siblings, 0, 0, tiled=True))  19.4 us
    all_to_all x1, blocking collectives, local(): back = held(lax.all_to_all(scanned, far, 0, 0, tiled=True))  15.4 us
    all_to_all x1, waiting for transfers between devices, local(): start = held(lax.all_to_all(starts, siblings, 0, 0, tiled=True))  6.94 us
    all_to_all x1, starting transfers between devices, local(): start = held(lax.all_to_all(starts, siblings, 0, 0, tiled=True))  6.6 us
    pallas_call x1, Pallas kernels, sums_call(): pl.pallas_call(sums_kernel, in_specs=[outside] * 3, out_shape=(near(SIB,...  2.77 us
    pallas_call x1, Pallas kernels, running_call(): pl.pallas_call(running_kernel, out_shape=(shape(M, R), shape(16, LANES, d...  2.25 us
    all_gather x1, blocking collectives, local(): closed = held(lax.all_gather(closing_half, 'c'))  1.9 us
  transfers between devices with their start and end apart: 1, of which 1 were waited for; matrix products, arithmetic and copies ran while one was open for 0% of the time, Pallas kernels for 1%

profile of v8, /device:TPU:1, one launch (start us, length us, event | category | flops | bytes accessed | tf_op | source)
XLA Modules:
  0.0 81.9 jit_solution(15707037284981905281)
XLA Ops:
  0.6 2.8 %local_sums.1 = (f32[8,136,128]{2,1,0:T(8,128)S(1)}, s32[16,128]{1,0:T(8,128)S(1)}, bf16[288,2048]{1,0:T(8,128)(2,1)S(1)}, s32[2048,128]{1,0:T(8,128)S(1)}) custom-call(f32[64,2048]{1,0:T(8,128)} %bitcast.8, s32[16,128]{1,0:T(8,128)} %bitcast.9, s32[16,128]{1,0:T(8,128)} %bitcast.10), custom_call_target="tpu_custom_call" | custom-call | tf_op jit(solution)/shard_map/local_sums/pallas_call | solution.py:247
  3.4 19.4 %all_to_all.20.arrived = f32[8,136,128]{2,1,0:T(8,128)S(1)} all-to-all(f32[8,136,128]{2,1,0:T(8,128)S(1)} %get-tuple-element.14), channel_id=1, replica_groups=mesh['y'=8,'z'=8,'c'=2,'x'=4] {'x','c'}, dimensions={0} | all-to-all | bytes 1114112 | tf_op jit(solution)/shard_map/all_to_all | solution.py:301
  22.8 0.1 slice_sums.1
  22.8 24.0 %all_to_all.21.arrived = f32[64,4,128]{2,1,0:T(4,128)S(1)} all-to-all(f32[64,4,128]{2,1,0:T(4,128)S(1)} %slice_sums.1), channel_id=1, replica_groups=mesh['y'=8,'z'=8,'c'=2,'x'=4] {'y','z'}, dimensions={0} | all-to-all | bytes 262144 | tf_op jit(solution)/shard_map/all_to_all | solution.py:310
  46.8 0.1 scan.1
  46.9 15.4 %all_to_all.22.far = f32[64,4,128]{2,1,0:T(4,128)S(1)} all-to-all(f32[64,4,128]{2,1,0:T(4,128)S(1)} %get-tuple-element.15), channel_id=1, replica_groups=mesh['y'=8,'z'=8,'c'=2,'x'=4] {'y','z'}, dimensions={0} | all-to-all | bytes 262144 | tf_op jit(solution)/shard_map/all_to_all | solution.py:317
  62.4 0.9 %starts.1 = (f32[8,136,128]{2,1,0:T(8,128)}, f32[128,128]{1,0:T(8,128)S(1)}) custom-call(f32[64,4,128]{2,1,0:T(4,128)S(1)} %all_to_all.22.far, f32[8,136,128]{2,1,0:T(8,128)S(1)} %all_to_all.20.arrived, f32[8,128]{1,0:T(8,128)S(1)} %get-tuple-element.16.counts), custom_call_target="tpu_custom_call" | custom-call | tf_op jit(solution)/shard_map/starts/pallas_call | solution.py:318
  63.3 6.6 %all-to-all-start.3 = ((f32[8,136,128]{2,1,0:T(8,128)}), f32[8,136,128]{2,1,0:T(8,128)S(1)}, u32[]{:S(2)}, u32[]{:S(2)}) async-start(f32[8,136,128]{2,1,0:T(8,128)} %get-tuple-element.17), calls=%async_computation.3 | async-start | bytes 1114112 | tf_op jit(solution)/shard_map/all_to_all | solution.py:332
  69.9 0.9 %own_rows.1.own = f32[72,2048]{1,0:T(8,128)S(1)} custom-call(bf16[288,2048]{1,0:T(8,128)(2,1)S(1)} %get-tuple-element.18.split, s32[16,128]{1,0:T(8,128)S(1)} %get-tuple-element.19.slot, s32[2048,128]{1,0:T(8,128)S(1)} %get-tuple-element.20.cols), custom_call_target="tpu_custom_call" | custom-call | flops 603979776 | bytes 1048576 | tf_op jit(solution)/shard_map/own_rows/pallas_call | solution.py:268
  70.8 1.9 %all-gather = f32[256,128]{1,0:T(8,128)S(1)} all-gather(f32[128,128]{1,0:T(8,128)S(1)} %get-tuple-element.21), channel_id=2, replica_groups=mesh['y'=8,'z'=8,'c'=2,'x'=4] {'c'}, dimensions={0}, use_global_device_ids=true | all-gather | bytes 196608 | tf_op jit(solution)/shard_map/all_gather | solution.py:330
  72.7 6.9 %all-to-all-done.3.start = f32[8,136,128]{2,1,0:T(8,128)S(1)} async-done(((f32[8,136,128]{2,1,0:T(8,128)}), f32[8,136,128]{2,1,0:T(8,128)S(1)}, u32[]{:S(2)}, u32[]{:S(2)}) %all-to-all-start.3) | async-done | bytes 557088 | tf_op jit(solution)/shard_map/all_to_all | solution.py:332
  79.6 2.2 %running_means.1 = (f32[64,2048]{1,0:T(8,128)}, s32[16,128]{1,0:T(8,128)}, f32[64,512]{1,0:T(8,128)}) custom-call(f32[8,136,128]{2,1,0:T(8,128)S(1)} %all-to-all-done.3.start, f32[72,2048]{1,0:T(8,128)S(1)} %own_rows.1.own, s32[16,128]{1,0:T(8,128)S(1)} %get-tuple-element.19.slot, f32[2,128,128]{2,1,0:T(8,128)S(1)} %bitcast.7), custom_call_target="tpu_custom_call" | custom-call | tf_op jit(solution)/shard_map/running_means/pallas_call | solution.py:279
Async XLA Ops:
  63.3 16.3 %all-to-all-start.3 = ((f32[8,136,128]{2,1,0:T(8,128)}), f32[8,136,128]{2,1,0:T(8,128)S(1)}, u32[]{:S(2)}, u32[]{:S(2)}) async-start(f32[8,136,128]{2,1,0:T(8,128)} %get-tuple-element.17), calls=%async_computation.3 | async-start | bytes 1114112 | tf_op jit(solution)/shard_map/all_to_all | solution.py:332

commit v9 on v8

--- a/solution.py
+++ b/solution.py
@@ -16,6 +16,9 @@
 T = 256
 NT = S // T
 NH = NT // 2
+WAYS = 4
+PART = S // WAYS
+NW = NT // WAYS
 SIB = 8
 FAR = 64
 MSG = 136
@@ -51,6 +54,10 @@
 
 def dot(a, b):
     return lax.dot_general(a, b, (((1,), (0,)), ((), ())), preferred_element_type=F32)
+
+
+def owner(block):
+    return 4 * (block % 2) + block // 2
 
 
 def hot(mask):
@@ -105,7 +112,7 @@
         for h in range(2):
             of = res[h * LHS : (h + 1) * LHS]
             total = of[0:64] + of[64:128]
-            to = h * NH + j
+            to = owner(h * NH + j)
             out[to, 0:64, :] = total[:, :LANES]
             out[to, 64:128, :] = total[:, LANES:]
             number = jnp.broadcast_to(of[128:129], (8, T))
@@ -148,11 +155,10 @@
     acc = buf[...]
     copies = []
     for k in range(SIB):
-        i = 2 * (k % 4) + k // 4
-        out[i] = acc
-        copies.append(pltpu.make_async_copy(out.at[i], out_far.at[i], sems.at[i]))
+        out[k] = acc
+        copies.append(pltpu.make_async_copy(out.at[k], out_far.at[k], sems.at[k]))
         copies[-1].start()
-        acc = acc + arrived[i]
+        acc = acc + arrived[k]
     for copy in copies:
         copy.wait()
 
@@ -190,23 +196,26 @@
     sub = lax.broadcasted_iota(jnp.int32, (16, LANES), 0)
     for j in range(NT):
         for h in range(2):
-            a, b, _ = pieces(start[j, h * 64 : (h + 1) * 64, :])
-            n = pieces(start[j, 128 + h : 129 + h, :])
+            a, b, _ = pieces(start[owner(j), h * 64 : (h + 1) * 64, :])
+            n = pieces(start[owner(j), 128 + h : 129 + h, :])
             n = [jnp.broadcast_to(v.astype(F32), (16, LANES)) for v in n]
             n = jnp.where(sub == 0, n[0], jnp.where(sub == 1, n[1], jnp.where(sub == 2, n[2], 0.0)))
-            top = (j // NH) * LHS
-            at = (j % NH) * T + h * LANES
+            top = (j // NW) * LHS
+            at = (j % NW) * T + h * LANES
             left[top : top + LHS, at : at + LANES] = jnp.concatenate([a, b, n.astype(BF16)], axis=0)
     label = lax.broadcasted_iota(jnp.int32, (T, T), 0)
     for j in range(NT):
         row = both(slot, j)
-        high = jnp.broadcast_to(row, (LHS, T)) >= HALF
-        low = jnp.bitwise_and(jnp.broadcast_to(row, (T, T)), HALF - 1)
+        high = jnp.broadcast_to(jnp.right_shift(row, 9), (LHS, T))
+        low = jnp.bitwise_and(jnp.broadcast_to(row, (T, T)), PART - 1)
         res = None
-        for k in range(NH):
+        for k in range(NW):
             part = dot(left[:, k * T : (k + 1) * T], hot(label + k * T == low))
             res = part if res is None else res + part
-        res = jnp.where(high, res[LHS : 2 * LHS], res[0:LHS])
+        found = res[0:LHS]
+        for w in range(1, WAYS):
+            found = jnp.where(high == w, res[w * LHS : (w + 1) * LHS], found)
+        res = found
         at = slice(j * T, (j + 1) * T)
         total = res[0:64] + res[64:128] + own[0:64, at]
         tally = (res[128:129] + res[129:130]) + res[130:131] + own[64:65, at]
@@ -281,7 +290,7 @@
         out_shape=(shape(M, R), shape(16, LANES, dtype=jnp.int32), shape(M, 512)),
         out_specs=(pl.BlockSpec(memory_space=pl.ANY),) * 3,
         scratch_shapes=[
-            pltpu.VMEM((2 * LHS, HALF), BF16),
+            pltpu.VMEM((WAYS * LHS, PART), BF16),
             pltpu.VMEM((M, R), F32),
             pltpu.VMEM((16, LANES), jnp.int32),
             pltpu.VMEM((M, 2 * T), F32),
@@ -297,7 +306,7 @@
     gid = group_ids.reshape(16, LANES)
     table = slot_of.reshape(16, LANES)
     sums, slot, split, cols = sums_call(vt, gid, table)
-    siblings = ("x", "c")
+    siblings = ("c", "x")
     arrived = held(lax.all_to_all(sums, siblings, 0, 0, tiled=True))
     far = ("y", "z")
     pieces_out = pl.pallas_call(

time: 82.2 us -> 82.2 us (level)
  no operation moved by 1% of the time
where the time goes in v9:
time: 82.2 us; the launch traced here: 81.9 us
  blocking collectives  60.8 us (74%)
  Pallas kernels  6.96 us (8%)
  waiting for transfers between devices  6.92 us (8%)
  starting transfers between devices  6.5 us (8%)
    all_to_all x1, blocking collectives, local(): met = held(lax.all_to_all(pieces_out, far, 0, 0, tiled=True))  24 us
    all_to_all x1, blocking collectives, local(): arrived = held(lax.all_to_all(sums, siblings, 0, 0, tiled=True))  19.4 us
    all_to_all x1, blocking collectives, local(): back = held(lax.all_to_all(scanned, far, 0, 0, tiled=True))  15.6 us
    all_to_all x1, waiting for transfers between devices, local(): start = held(lax.all_to_all(starts, siblings, 0, 0, tiled=True))  6.92 us
    all_to_all x1, starting transfers between devices, local(): start = held(lax.all_to_all(starts, siblings, 0, 0, tiled=True))  6.5 us
    pallas_call x1, Pallas kernels, sums_call(): pl.pallas_call(sums_kernel, in_specs=[outside] * 3, out_shape=(near(SIB,...  2.77 us
    pallas_call x1, Pallas kernels, running_call(): pl.pallas_call(running_kernel, out_shape=(shape(M, R), shape(16, LANES, d...  2.22 us
    all_gather x1, blocking collectives, local(): closed = held(lax.all_gather(closing_half, 'c'))  1.9 us
  transfers between devices with their start and end apart: 1, of which 1 were waited for; matrix products, arithmetic and copies ran while one was open for 0% of the time, Pallas kernels for 1%

profile of v9, /device:TPU:1, one launch (start us, length us, event | category | flops | bytes accessed | tf_op | source)
XLA Modules:
  0.0 81.9 jit_solution(7467208370405829902)
XLA Ops:
  0.6 2.8 %local_sums.1 = (f32[8,136,128]{2,1,0:T(8,128)S(1)}, s32[16,128]{1,0:T(8,128)S(1)}, bf16[288,2048]{1,0:T(8,128)(2,1)S(1)}, s32[2048,128]{1,0:T(8,128)S(1)}) custom-call(f32[64,2048]{1,0:T(8,128)} %bitcast.8, s32[16,128]{1,0:T(8,128)} %bitcast.9, s32[16,128]{1,0:T(8,128)} %bitcast.10), custom_call_target="tpu_custom_call" | custom-call | tf_op jit(solution)/shard_map/local_sums/pallas_call | solution.py:256
  3.4 19.4 %all_to_all.20.arrived = f32[8,136,128]{2,1,0:T(8,128)S(1)} all-to-all(f32[8,136,128]{2,1,0:T(8,128)S(1)} %get-tuple-element.14), channel_id=1, replica_groups=mesh['y'=8,'z'=8,'c'=2,'x'=4] {'c','x'}, dimensions={0} | all-to-all | bytes 1114112 | tf_op jit(solution)/shard_map/all_to_all | solution.py:310
  22.8 0.1 slice_sums.1
  22.8 24.0 %all_to_all.21.arrived = f32[64,4,128]{2,1,0:T(4,128)S(1)} all-to-all(f32[64,4,128]{2,1,0:T(4,128)S(1)} %slice_sums.1), channel_id=1, replica_groups=mesh['y'=8,'z'=8,'c'=2,'x'=4] {'y','z'}, dimensions={0} | all-to-all | bytes 262144 | tf_op jit(solution)/shard_map/all_to_all | solution.py:319
  46.8 0.1 scan.1
  46.9 15.6 %all_to_all.22.far = f32[64,4,128]{2,1,0:T(4,128)S(1)} all-to-all(f32[64,4,128]{2,1,0:T(4,128)S(1)} %get-tuple-element.15), channel_id=1, replica_groups=mesh['y'=8,'z'=8,'c'=2,'x'=4] {'y','z'}, dimensions={0} | all-to-all | bytes 262144 | tf_op jit(solution)/shard_map/all_to_all | solution.py:326
  62.5 0.9 %starts.1 = (f32[8,136,128]{2,1,0:T(8,128)}, f32[128,128]{1,0:T(8,128)S(1)}) custom-call(f32[64,4,128]{2,1,0:T(4,128)S(1)} %all_to_all.22.far, f32[8,136,128]{2,1,0:T(8,128)S(1)} %all_to_all.20.arrived, f32[8,128]{1,0:T(8,128)S(1)} %get-tuple-element.16.counts), custom_call_target="tpu_custom_call" | custom-call | tf_op jit(solution)/shard_map/starts/pallas_call | solution.py:327
  63.4 6.5 %all-to-all-start.3 = ((f32[8,136,128]{2,1,0:T(8,128)}), f32[8,136,128]{2,1,0:T(8,128)S(1)}, u32[]{:S(2)}, u32[]{:S(2)}) async-start(f32[8,136,128]{2,1,0:T(8,128)} %get-tuple-element.17), calls=%async_computation.3 | async-start | bytes 1114112 | tf_op jit(solution)/shard_map/all_to_all | solution.py:341
  69.9 0.9 %own_rows.1.own = f32[72,2048]{1,0:T(8,128)S(1)} custom-call(bf16[288,2048]{1,0:T(8,128)(2,1)S(1)} %get-tuple-element.18.split, s32[16,128]{1,0:T(8,128)S(1)} %get-tuple-element.19.slot, s32[2048,128]{1,0:T(8,128)S(1)} %get-tuple-element.20.cols), custom_call_target="tpu_custom_call" | custom-call | flops 603979776 | bytes 1048576 | tf_op jit(solution)/shard_map/own_rows/pallas_call | solution.py:277
  70.8 1.9 %all-gather = f32[256,128]{1,0:T(8,128)S(1)} all-gather(f32[128,128]{1,0:T(8,128)S(1)} %get-tuple-element.21), channel_id=2, replica_groups=mesh['y'=8,'z'=8,'c'=2,'x'=4] {'c'}, dimensions={0}, use_global_device_ids=true | all-gather | bytes 196608 | tf_op jit(solution)/shard_map/all_gather | solution.py:339
  72.7 6.9 %all-to-all-done.3.start = f32[8,136,128]{2,1,0:T(8,128)S(1)} async-done(((f32[8,136,128]{2,1,0:T(8,128)}), f32[8,136,128]{2,1,0:T(8,128)S(1)}, u32[]{:S(2)}, u32[]{:S(2)}) %all-to-all-start.3) | async-done | bytes 557088 | tf_op jit(solution)/shard_map/all_to_all | solution.py:341
  79.6 2.2 %running_means.1 = (f32[64,2048]{1,0:T(8,128)}, s32[16,128]{1,0:T(8,128)}, f32[64,512]{1,0:T(8,128)}) custom-call(f32[8,136,128]{2,1,0:T(8,128)S(1)} %all-to-all-done.3.start, f32[72,2048]{1,0:T(8,128)S(1)} %own_rows.1.own, s32[16,128]{1,0:T(8,128)S(1)} %get-tuple-element.19.slot, f32[2,128,128]{2,1,0:T(8,128)S(1)} %bitcast.7), custom_call_target="tpu_custom_call" | custom-call | tf_op jit(solution)/shard_map/running_means/pallas_call | solution.py:288
Async XLA Ops:
  63.4 16.2 %all-to-all-start.3 = ((f32[8,136,128]{2,1,0:T(8,128)}), f32[8,136,128]{2,1,0:T(8,128)S(1)}, u32[]{:S(2)}, u32[]{:S(2)}) async-start(f32[8,136,128]{2,1,0:T(8,128)} %get-tuple-element.17), calls=%async_computation.3 | async-start | bytes 1114112 | tf_op jit(solution)/shard_map/all_to_all | solution.py:341

commit v10 on v9

--- a/solution.py
+++ b/solution.py
@@ -131,15 +131,18 @@
 
 
 def scan_kernel(arrived, out, counts_out):
-    mine = lax.axis_index("y") * 8 + lax.axis_index("z")
+    y = lax.axis_index("y")
+    z = lax.axis_index("z")
+    mine = y * 8 + z
     acc = jnp.zeros((4, LANES), F32)
     before = jnp.zeros((4, LANES), F32)
-    for p in range(FAR):
+    for r in range(FAR):
+        p = 8 * (r % 8) + r // 8
         got = arrived[p]
         out[p, 0:2, :] = acc[0:2]
-        before = before + jnp.where(p < mine, got, 0.0)
+        before = before + jnp.where(r < mine, got, 0.0)
         acc = acc + got
-    number = jnp.where(mine < FAR // 2, acc[2:3], acc[3:4])
+    number = jnp.where(z < 4, acc[2:3], acc[3:4])
     closing = acc[0:2] / jnp.maximum(number, 1.0)
     for p in range(FAR):
         out[p, 2:4, :] = closing
@@ -308,7 +311,7 @@
     sums, slot, split, cols = sums_call(vt, gid, table)
     siblings = ("c", "x")
     arrived = held(lax.all_to_all(sums, siblings, 0, 0, tiled=True))
-    far = ("y", "z")
+    far = ("z", "y")
     pieces_out = pl.pallas_call(
         slice_kernel,
         out_shape=near(FAR, 4, LANES),

time: 82.2 us -> 82.1 us (level)
  no operation moved by 1% of the time
where the time goes in v10:
time: 82.1 us; the launch traced here: 81.8 us
  blocking collectives  61 us (74%)
  Pallas kernels  6.96 us (8%)
  waiting for transfers between devices  6.92 us (8%)
  starting transfers between devices  6.26 us (8%)
    all_to_all x1, blocking collectives, local(): met = held(lax.all_to_all(pieces_out, far, 0, 0, tiled=True))  24 us
    all_to_all x1, blocking collectives, local(): arrived = held(lax.all_to_all(sums, siblings, 0, 0, tiled=True))  19.4 us
    all_to_all x1, blocking collectives, local(): back = held(lax.all_to_all(scanned, far, 0, 0, tiled=True))  15.7 us
    all_to_all x1, waiting for transfers between devices, local(): start = held(lax.all_to_all(starts, siblings, 0, 0, tiled=True))  6.92 us
    all_to_all x1, starting transfers between devices, local(): start = held(lax.all_to_all(starts, siblings, 0, 0, tiled=True))  6.26 us
    pallas_call x1, Pallas kernels, sums_call(): pl.pallas_call(sums_kernel, in_specs=[outside] * 3, out_shape=(near(SIB,...  2.77 us
    pallas_call x1, Pallas kernels, running_call(): pl.pallas_call(running_kernel, out_shape=(shape(M, R), shape(16, LANES, d...  2.22 us
    all_gather x1, blocking collectives, local(): closed = held(lax.all_gather(closing_half, 'c'))  1.9 us
  transfers between devices with their start and end apart: 1, of which 1 were waited for; matrix products, arithmetic and copies ran while one was open for 0% of the time, Pallas kernels for 1%

profile of v10, /device:TPU:1, one launch (start us, length us, event | category | flops | bytes accessed | tf_op | source)
XLA Modules:
  0.0 81.8 jit_solution(6011823434775804173)
XLA Ops:
  0.6 2.8 %local_sums.1 = (f32[8,136,128]{2,1,0:T(8,128)S(1)}, s32[16,128]{1,0:T(8,128)S(1)}, bf16[288,2048]{1,0:T(8,128)(2,1)S(1)}, s32[2048,128]{1,0:T(8,128)S(1)}) custom-call(f32[64,2048]{1,0:T(8,128)} %bitcast.8, s32[16,128]{1,0:T(8,128)} %bitcast.9, s32[16,128]{1,0:T(8,128)} %bitcast.10), custom_call_target="tpu_custom_call" | custom-call | tf_op jit(solution)/shard_map/local_sums/pallas_call | solution.py:259
  3.4 19.4 %all_to_all.20.arrived = f32[8,136,128]{2,1,0:T(8,128)S(1)} all-to-all(f32[8,136,128]{2,1,0:T(8,128)S(1)} %get-tuple-element.14), channel_id=1, replica_groups=mesh['y'=8,'z'=8,'c'=2,'x'=4] {'c','x'}, dimensions={0} | all-to-all | bytes 1114112 | tf_op jit(solution)/shard_map/all_to_all | solution.py:313
  22.8 0.1 slice_sums.1
  22.8 24.0 %all_to_all.21.arrived = f32[64,4,128]{2,1,0:T(4,128)S(1)} all-to-all(f32[64,4,128]{2,1,0:T(4,128)S(1)} %slice_sums.1), channel_id=1, replica_groups=mesh['y'=8,'z'=8,'c'=2,'x'=4] {'z','y'}, dimensions={0} | all-to-all | bytes 262144 | tf_op jit(solution)/shard_map/all_to_all | solution.py:322
  46.9 0.1 scan.1
  47.0 15.7 %all_to_all.22.far = f32[64,4,128]{2,1,0:T(4,128)S(1)} all-to-all(f32[64,4,128]{2,1,0:T(4,128)S(1)} %get-tuple-element.15), channel_id=1, replica_groups=mesh['y'=8,'z'=8,'c'=2,'x'=4] {'z','y'}, dimensions={0} | all-to-all | bytes 262144 | tf_op jit(solution)/shard_map/all_to_all | solution.py:329
  62.7 0.9 %starts.1 = (f32[8,136,128]{2,1,0:T(8,128)}, f32[128,128]{1,0:T(8,128)S(1)}) custom-call(f32[64,4,128]{2,1,0:T(4,128)S(1)} %all_to_all.22.far, f32[8,136,128]{2,1,0:T(8,128)S(1)} %all_to_all.20.arrived, f32[8,128]{1,0:T(8,128)S(1)} %get-tuple-element.16.counts), custom_call_target="tpu_custom_call" | custom-call | tf_op jit(solution)/shard_map/starts/pallas_call | solution.py:330
  63.6 6.3 %all-to-all-start.3 = ((f32[8,136,128]{2,1,0:T(8,128)}), f32[8,136,128]{2,1,0:T(8,128)S(1)}, u32[]{:S(2)}, u32[]{:S(2)}) async-start(f32[8,136,128]{2,1,0:T(8,128)} %get-tuple-element.17), calls=%async_computation.3 | async-start | bytes 1114112 | tf_op jit(solution)/shard_map/all_to_all | solution.py:344
  69.9 0.9 %own_rows.1.own = f32[72,2048]{1,0:T(8,128)S(1)} custom-call(bf16[288,2048]{1,0:T(8,128)(2,1)S(1)} %get-tuple-element.18.split, s32[16,128]{1,0:T(8,128)S(1)} %get-tuple-element.19.slot, s32[2048,128]{1,0:T(8,128)S(1)} %get-tuple-element.20.cols), custom_call_target="tpu_custom_call" | custom-call | flops 603979776 | bytes 1048576 | tf_op jit(solution)/shard_map/own_rows/pallas_call | solution.py:280
  70.8 1.9 %all-gather = f32[256,128]{1,0:T(8,128)S(1)} all-gather(f32[128,128]{1,0:T(8,128)S(1)} %get-tuple-element.21), channel_id=2, replica_groups=mesh['y'=8,'z'=8,'c'=2,'x'=4] {'c'}, dimensions={0}, use_global_device_ids=true | all-gather | bytes 196608 | tf_op jit(solution)/shard_map/all_gather | solution.py:342
  72.7 6.9 %all-to-all-done.3.start = f32[8,136,128]{2,1,0:T(8,128)S(1)} async-done(((f32[8,136,128]{2,1,0:T(8,128)}), f32[8,136,128]{2,1,0:T(8,128)S(1)}, u32[]{:S(2)}, u32[]{:S(2)}) %all-to-all-start.3) | async-done | bytes 557088 | tf_op jit(solution)/shard_map/all_to_all | solution.py:344
  79.6 2.2 %running_means.1 = (f32[64,2048]{1,0:T(8,128)}, s32[16,128]{1,0:T(8,128)}, f32[64,512]{1,0:T(8,128)}) custom-call(f32[8,136,128]{2,1,0:T(8,128)S(1)} %all-to-all-done.3.start, f32[72,2048]{1,0:T(8,128)S(1)} %own_rows.1.own, s32[16,128]{1,0:T(8,128)S(1)} %get-tuple-element.19.slot, f32[2,128,128]{2,1,0:T(8,128)S(1)} %bitcast.7), custom_call_target="tpu_custom_call" | custom-call | tf_op jit(solution)/shard_map/running_means/pallas_call | solution.py:291
Async XLA Ops:
  63.6 16.0 %all-to-all-start.3 = ((f32[8,136,128]{2,1,0:T(8,128)}), f32[8,136,128]{2,1,0:T(8,128)S(1)}, u32[]{:S(2)}, u32[]{:S(2)}) async-start(f32[8,136,128]{2,1,0:T(8,128)} %get-tuple-element.17), calls=%async_computation.3 | async-start | bytes 1114112 | tf_op jit(solution)/shard_map/all_to_all | solution.py:344

commit v11 on v7

--- a/solution.py
+++ b/solution.py
@@ -16,6 +16,9 @@
 T = 256
 NT = S // T
 NH = NT // 2
+WAYS = 4
+PART = S // WAYS
+NW = NT // WAYS
 SIB = 8
 RING = 8
 MSG = 136
@@ -51,6 +54,10 @@
 
 def dot(a, b):
     return lax.dot_general(a, b, (((1,), (0,)), ((), ())), preferred_element_type=F32)
+
+
+def owner(block):
+    return 4 * (block % 2) + block // 2
 
 
 def hot(mask):
@@ -105,7 +112,7 @@
         for h in range(2):
             of = res[h * LHS : (h + 1) * LHS]
             total = of[0:64] + of[64:128]
-            to = h * NH + j
+            to = owner(h * NH + j)
             out[to, 0:64, :] = total[:, :LANES]
             out[to, 64:128, :] = total[:, LANES:]
             number = jnp.broadcast_to(of[128:129], (8, T))
@@ -158,11 +165,10 @@
     acc = jnp.concatenate(parts + [counts[...]], axis=0)
     copies = []
     for k in range(SIB):
-        i = 2 * (k % 4) + k // 4
-        out[i] = acc
-        copies.append(pltpu.make_async_copy(out.at[i], out_far.at[i], sems.at[i]))
+        out[k] = acc
+        copies.append(pltpu.make_async_copy(out.at[k], out_far.at[k], sems.at[k]))
         copies[-1].start()
-        acc = acc + arrived[i]
+        acc = acc + arrived[k]
     for copy in copies:
         copy.wait()
 
@@ -200,23 +206,26 @@
     sub = lax.broadcasted_iota(jnp.int32, (16, LANES), 0)
     for j in range(NT):
         for h in range(2):
-            a, b, _ = pieces(start[j, h * 64 : (h + 1) * 64, :])
-            n = pieces(start[j, 128 + h : 129 + h, :])
+            a, b, _ = pieces(start[owner(j), h * 64 : (h + 1) * 64, :])
+            n = pieces(start[owner(j), 128 + h : 129 + h, :])
             n = [jnp.broadcast_to(v.astype(F32), (16, LANES)) for v in n]
             n = jnp.where(sub == 0, n[0], jnp.where(sub == 1, n[1], jnp.where(sub == 2, n[2], 0.0)))
-            top = (j // NH) * LHS
-            at = (j % NH) * T + h * LANES
+            top = (j // NW) * LHS
+            at = (j % NW) * T + h * LANES
             left[top : top + LHS, at : at + LANES] = jnp.concatenate([a, b, n.astype(BF16)], axis=0)
     label = lax.broadcasted_iota(jnp.int32, (T, T), 0)
     for j in range(NT):
         row = both(slot, j)
-        high = jnp.broadcast_to(row, (LHS, T)) >= HALF
-        low = jnp.bitwise_and(jnp.broadcast_to(row, (T, T)), HALF - 1)
+        high = jnp.broadcast_to(jnp.right_shift(row, 9), (LHS, T))
+        low = jnp.bitwise_and(jnp.broadcast_to(row, (T, T)), PART - 1)
         res = None
-        for k in range(NH):
+        for k in range(NW):
             part = dot(left[:, k * T : (k + 1) * T], hot(label + k * T == low))
             res = part if res is None else res + part
-        res = jnp.where(high, res[LHS : 2 * LHS], res[0:LHS])
+        found = res[0:LHS]
+        for w in range(1, WAYS):
+            found = jnp.where(high == w, res[w * LHS : (w + 1) * LHS], found)
+        res = found
         at = slice(j * T, (j + 1) * T)
         total = res[0:64] + res[64:128] + own[0:64, at]
         tally = (res[128:129] + res[129:130]) + res[130:131] + own[64:65, at]
@@ -291,7 +300,7 @@
         out_shape=(shape(M, R), shape(16, LANES, dtype=jnp.int32), shape(M, 512)),
         out_specs=(pl.BlockSpec(memory_space=pl.ANY),) * 3,
         scratch_shapes=[
-            pltpu.VMEM((2 * LHS, HALF), BF16),
+            pltpu.VMEM((WAYS * LHS, PART), BF16),
             pltpu.VMEM((M, R), F32),
             pltpu.VMEM((16, LANES), jnp.int32),
             pltpu.VMEM((M, 2 * T), F32),
@@ -307,7 +316,7 @@
     gid = group_ids.reshape(16, LANES)
     table = slot_of.reshape(16, LANES)
     sums, slot, split, cols = sums_call(vt, gid, table)
-    siblings = ("x", "c")
+    siblings = ("c", "x")
     arrived = held(lax.all_to_all(sums, siblings, 0, 0, tiled=True))
     parts = pl.pallas_call(
         slice_kernel,

time: 82.4 us -> 82.2 us (level)
  no operation moved by 1% of the time
where the time goes in v11:
time: 82.2 us; the launch traced here: 81.9 us
  blocking collectives  59.5 us (72%)
  starting transfers between devices  7.95 us (10%)
  waiting for transfers between devices  6.92 us (8%)
  Pallas kernels  6.83 us (8%)
    all_to_all x1, blocking collectives, local(): arrived = held(lax.all_to_all(sums, siblings, 0, 0, tiled=True))  19.4 us
    all_to_all x1, blocking collectives, local(): along_y = held(lax.all_to_all(ring, 'y', 0, 0, tiled=True))  14.2 us
    all_to_all x1, blocking collectives, local(): along_z = held(lax.all_to_all(parts, 'z', 0, 0, tiled=True))  13.7 us
    all_to_all x1, blocking collectives, local(): back = held(lax.all_to_all(scanned, 'z', 0, 0, tiled=True))  10.4 us
    all_to_all x1, starting transfers between devices, local(): start = held(lax.all_to_all(starts, siblings, 0, 0, tiled=True))  7.95 us
    all_to_all x1, waiting for transfers between devices, local(): start = held(lax.all_to_all(starts, siblings, 0, 0, tiled=True))  6.92 us
    pallas_call x1, Pallas kernels, sums_call(): pl.pallas_call(sums_kernel, in_specs=[outside] * 3, out_shape=(near(SIB,...  2.77 us
    pallas_call x1, Pallas kernels, running_call(): pl.pallas_call(running_kernel, out_shape=(shape(M, R), shape(16, LANES, d...  2.22 us
  transfers between devices with their start and end apart: 1, of which 1 were waited for; matrix products, arithmetic and copies ran while one was open for 0% of the time, Pallas kernels for 1%

profile of v11, /device:TPU:1, one launch (start us, length us, event | category | flops | bytes accessed | tf_op | source)
XLA Modules:
  0.0 81.9 jit_solution(14570558030469392480)
XLA Ops:
  0.6 2.8 %local_sums.1 = (f32[8,136,128]{2,1,0:T(8,128)S(1)}, s32[16,128]{1,0:T(8,128)S(1)}, bf16[288,2048]{1,0:T(8,128)(2,1)S(1)}, s32[2048,128]{1,0:T(8,128)S(1)}) custom-call(f32[64,2048]{1,0:T(8,128)} %bitcast.8, s32[16,128]{1,0:T(8,128)} %bitcast.9, s32[16,128]{1,0:T(8,128)} %bitcast.10), custom_call_target="tpu_custom_call" | custom-call | tf_op jit(solution)/shard_map/local_sums/pallas_call | solution.py:266
  3.4 19.4 %all_to_all.25.arrived = f32[8,136,128]{2,1,0:T(8,128)S(1)} all-to-all(f32[8,136,128]{2,1,0:T(8,128)S(1)} %get-tuple-element.14), channel_id=1, replica_groups=mesh['y'=8,'z'=8,'c'=2,'x'=4] {'c','x'}, dimensions={0} | all-to-all | bytes 1114112 | tf_op jit(solution)/shard_map/all_to_all | solution.py:320
  22.8 13.7 %all_to_all.26.arrived = f32[8,24,128]{2,1,0:T(8,128)S(1)} all-to-all(f32[8,24,128]{2,1,0:T(8,128)S(1)} %slice_sums.1), channel_id=1, replica_groups=mesh['y'=8,'z'=8,'c'=2,'x'=4] {'z'}, dimensions={0} | all-to-all | bytes 196608 | tf_op jit(solution)/shard_map/all_to_all | solution.py:327
  36.5 14.2 %all_to_all.27.rings = f32[8,24,128]{2,1,0:T(8,128)S(1)} all-to-all(f32[8,24,128]{2,1,0:T(8,128)S(1)} %ring_sums.1), channel_id=1, replica_groups=mesh['y'=8,'z'=8,'c'=2,'x'=4] {'y'}, dimensions={0} | all-to-all | bytes 196608 | tf_op jit(solution)/shard_map/all_to_all | solution.py:334
  50.7 10.4 %all_to_all.28.far = f32[8,32,128]{2,1,0:T(8,128)S(1)} all-to-all(f32[8,32,128]{2,1,0:T(8,128)S(1)} %get-tuple-element.15), channel_id=1, replica_groups=mesh['y'=8,'z'=8,'c'=2,'x'=4] {'z'}, dimensions={0} | all-to-all | bytes 262144 | tf_op jit(solution)/shard_map/all_to_all | solution.py:341
  61.1 0.9 %starts.1 = (f32[8,136,128]{2,1,0:T(8,128)}, f32[128,128]{1,0:T(8,128)S(1)}) custom-call(f32[8,32,128]{2,1,0:T(8,128)S(1)} %all_to_all.28.far, f32[8,136,128]{2,1,0:T(8,128)S(1)} %all_to_all.25.arrived, f32[8,128]{1,0:T(8,128)S(1)} %get-tuple-element.16.counts), custom_call_target="tpu_custom_call" | custom-call | tf_op jit(solution)/shard_map/starts/pallas_call | solution.py:342
  62.0 7.9 %all-to-all-start.4 = ((f32[8,136,128]{2,1,0:T(8,128)}), f32[8,136,128]{2,1,0:T(8,128)S(1)}, u32[]{:S(2)}, u32[]{:S(2)}) async-start(f32[8,136,128]{2,1,0:T(8,128)} %get-tuple-element.17), calls=%async_computation.4 | async-start | bytes 1114112 | tf_op jit(solution)/shard_map/all_to_all | solution.py:352
  70.0 0.9 %own_rows.1.own = f32[72,2048]{1,0:T(8,128)S(1)} custom-call(bf16[288,2048]{1,0:T(8,128)(2,1)S(1)} %get-tuple-element.18.split, s32[16,128]{1,0:T(8,128)S(1)} %get-tuple-element.19.slot, s32[2048,128]{1,0:T(8,128)S(1)} %get-tuple-element.20.cols), custom_call_target="tpu_custom_call" | custom-call | flops 603979776 | bytes 1048576 | tf_op jit(solution)/shard_map/own_rows/pallas_call | solution.py:287
  70.8 1.9 %all-gather = f32[256,128]{1,0:T(8,128)S(1)} all-gather(f32[128,128]{1,0:T(8,128)S(1)} %get-tuple-element.21), channel_id=2, replica_groups=mesh['y'=8,'z'=8,'c'=2,'x'=4] {'c'}, dimensions={0}, use_global_device_ids=true | all-gather | bytes 196608 | tf_op jit(solution)/shard_map/all_gather | solution.py:350
  72.7 6.9 %all-to-all-done.4.start = f32[8,136,128]{2,1,0:T(8,128)S(1)} async-done(((f32[8,136,128]{2,1,0:T(8,128)}), f32[8,136,128]{2,1,0:T(8,128)S(1)}, u32[]{:S(2)}, u32[]{:S(2)}) %all-to-all-start.4) | async-done | bytes 557088 | tf_op jit(solution)/shard_map/all_to_all | solution.py:352
  79.7 2.2 %running_means.1 = (f32[64,2048]{1,0:T(8,128)}, s32[16,128]{1,0:T(8,128)}, f32[64,512]{1,0:T(8,128)}) custom-call(f32[8,136,128]{2,1,0:T(8,128)S(1)} %all-to-all-done.4.start, f32[72,2048]{1,0:T(8,128)S(1)} %own_rows.1.own, s32[16,128]{1,0:T(8,128)S(1)} %get-tuple-element.19.slot, f32[2,128,128]{2,1,0:T(8,128)S(1)} %bitcast.7), custom_call_target="tpu_custom_call" | custom-call | tf_op jit(solution)/shard_map/running_means/pallas_call | solution.py:298
  (3 shorter events, 0.1 us)
Async XLA Ops:
  62.0 17.7 %all-to-all-start.4 = ((f32[8,136,128]{2,1,0:T(8,128)}), f32[8,136,128]{2,1,0:T(8,128)S(1)}, u32[]{:S(2)}, u32[]{:S(2)}) async-start(f32[8,136,128]{2,1,0:T(8,128)} %get-tuple-element.17), calls=%async_computation.4 | async-start | bytes 1114112 | tf_op jit(solution)/shard_map/all_to_all | solution.py:352

commit v12 on v9

--- a/solution.py
+++ b/solution.py
@@ -149,7 +149,6 @@
 def start_kernel(far, arrived, counts, out_far, closing, out, buf, sems):
     for p in range(FAR):
         buf[2 * p : 2 * p + 2, :] = far[p, 0:2, :]
-        closing[2 * p : 2 * p + 2, :] = far[p, 2:4, :]
     buf[128:130, :] = counts[0:2, :]
     buf[130:136, :] = jnp.zeros((6, LANES), F32)
     acc = buf[...]
@@ -159,6 +158,8 @@
         copies.append(pltpu.make_async_copy(out.at[k], out_far.at[k], sems.at[k]))
         copies[-1].start()
         acc = acc + arrived[k]
+    for p in range(FAR):
+        closing[2 * p : 2 * p + 2, :] = far[p, 2:4, :]
     for copy in copies:
         copy.wait()
 

time: 82.2 us -> 82.2 us (level)
  no operation moved by 1% of the time
where the time goes in v12:
time: 82.2 us; the launch traced here: 81.8 us
  blocking collectives  60.8 us (74%)
  Pallas kernels  6.93 us (8%)
  waiting for transfers between devices  6.93 us (8%)
  starting transfers between devices  6.5 us (8%)
    all_to_all x1, blocking collectives, local(): met = held(lax.all_to_all(pieces_out, far, 0, 0, tiled=True))  24 us
    all_to_all x1, blocking collectives, local(): arrived = held(lax.all_to_all(sums, siblings, 0, 0, tiled=True))  19.4 us
    all_to_all x1, blocking collectives, local(): back = held(lax.all_to_all(scanned, far, 0, 0, tiled=True))  15.6 us
    all_to_all x1, waiting for transfers between devices, local(): start = held(lax.all_to_all(starts, siblings, 0, 0, tiled=True))  6.93 us
    all_to_all x1, starting transfers between devices, local(): start = held(lax.all_to_all(starts, siblings, 0, 0, tiled=True))  6.5 us
    pallas_call x1, Pallas kernels, sums_call(): pl.pallas_call(sums_kernel, in_specs=[outside] * 3, out_shape=(near(SIB,...  2.77 us
    pallas_call x1, Pallas kernels, running_call(): pl.pallas_call(running_kernel, out_shape=(shape(M, R), shape(16, LANES, d...  2.22 us
    all_gather x1, blocking collectives, local(): closed = held(lax.all_gather(closing_half, 'c'))  1.9 us
  transfers between devices with their start and end apart: 1, of which 1 were waited for; matrix products, arithmetic and copies ran while one was open for 0% of the time, Pallas kernels for 1%

profile of v12, /device:TPU:1, one launch (start us, length us, event | category | flops | bytes accessed | tf_op | source)
XLA Modules:
  0.0 81.8 jit_solution(11215848122414464918)
XLA Ops:
  0.6 2.8 %local_sums.1 = (f32[8,136,128]{2,1,0:T(8,128)S(1)}, s32[16,128]{1,0:T(8,128)S(1)}, bf16[288,2048]{1,0:T(8,128)(2,1)S(1)}, s32[2048,128]{1,0:T(8,128)S(1)}) custom-call(f32[64,2048]{1,0:T(8,128)} %bitcast.8, s32[16,128]{1,0:T(8,128)} %bitcast.9, s32[16,128]{1,0:T(8,128)} %bitcast.10), custom_call_target="tpu_custom_call" | custom-call | tf_op jit(solution)/shard_map/local_sums/pallas_call | solution.py:257
  3.4 19.4 %all_to_all.20.arrived = f32[8,136,128]{2,1,0:T(8,128)S(1)} all-to-all(f32[8,136,128]{2,1,0:T(8,128)S(1)} %get-tuple-element.14), channel_id=1, replica_groups=mesh['y'=8,'z'=8,'c'=2,'x'=4] {'c','x'}, dimensions={0} | all-to-all | bytes 1114112 | tf_op jit(solution)/shard_map/all_to_all | solution.py:311
  22.8 0.1 slice_sums.1
  22.8 24.0 %all_to_all.21.arrived = f32[64,4,128]{2,1,0:T(4,128)S(1)} all-to-all(f32[64,4,128]{2,1,0:T(4,128)S(1)} %slice_sums.1), channel_id=1, replica_groups=mesh['y'=8,'z'=8,'c'=2,'x'=4] {'y','z'}, dimensions={0} | all-to-all | bytes 262144 | tf_op jit(solution)/shard_map/all_to_all | solution.py:320
  46.8 0.1 scan.1
  46.9 15.6 %all_to_all.22.far = f32[64,4,128]{2,1,0:T(4,128)S(1)} all-to-all(f32[64,4,128]{2,1,0:T(4,128)S(1)} %get-tuple-element.15), channel_id=1, replica_groups=mesh['y'=8,'z'=8,'c'=2,'x'=4] {'y','z'}, dimensions={0} | all-to-all | bytes 262144 | tf_op jit(solution)/shard_map/all_to_all | solution.py:327
  62.5 0.9 %starts.1 = (f32[8,136,128]{2,1,0:T(8,128)}, f32[128,128]{1,0:T(8,128)S(1)}) custom-call(f32[64,4,128]{2,1,0:T(4,128)S(1)} %all_to_all.22.far, f32[8,136,128]{2,1,0:T(8,128)S(1)} %all_to_all.20.arrived, f32[8,128]{1,0:T(8,128)S(1)} %get-tuple-element.16.counts), custom_call_target="tpu_custom_call" | custom-call | tf_op jit(solution)/shard_map/starts/pallas_call | solution.py:328
  63.4 6.5 %all-to-all-start.3 = ((f32[8,136,128]{2,1,0:T(8,128)}), f32[8,136,128]{2,1,0:T(8,128)S(1)}, u32[]{:S(2)}, u32[]{:S(2)}) async-start(f32[8,136,128]{2,1,0:T(8,128)} %get-tuple-element.17), calls=%async_computation.3 | async-start | bytes 1114112 | tf_op jit(solution)/shard_map/all_to_all | solution.py:342
  69.9 0.9 %own_rows.1.own = f32[72,2048]{1,0:T(8,128)S(1)} custom-call(bf16[288,2048]{1,0:T(8,128)(2,1)S(1)} %get-tuple-element.18.split, s32[16,128]{1,0:T(8,128)S(1)} %get-tuple-element.19.slot, s32[2048,128]{1,0:T(8,128)S(1)} %get-tuple-element.20.cols), custom_call_target="tpu_custom_call" | custom-call | flops 603979776 | bytes 1048576 | tf_op jit(solution)/shard_map/own_rows/pallas_call | solution.py:278
  70.8 1.9 %all-gather = f32[256,128]{1,0:T(8,128)S(1)} all-gather(f32[128,128]{1,0:T(8,128)S(1)} %get-tuple-element.21), channel_id=2, replica_groups=mesh['y'=8,'z'=8,'c'=2,'x'=4] {'c'}, dimensions={0}, use_global_device_ids=true | all-gather | bytes 196608 | tf_op jit(solution)/shard_map/all_gather | solution.py:340
  72.7 6.9 %all-to-all-done.3.start = f32[8,136,128]{2,1,0:T(8,128)S(1)} async-done(((f32[8,136,128]{2,1,0:T(8,128)}), f32[8,136,128]{2,1,0:T(8,128)S(1)}, u32[]{:S(2)}, u32[]{:S(2)}) %all-to-all-start.3) | async-done | bytes 557088 | tf_op jit(solution)/shard_map/all_to_all | solution.py:342
  79.6 2.2 %running_means.1 = (f32[64,2048]{1,0:T(8,128)}, s32[16,128]{1,0:T(8,128)}, f32[64,512]{1,0:T(8,128)}) custom-call(f32[8,136,128]{2,1,0:T(8,128)S(1)} %all-to-all-done.3.start, f32[72,2048]{1,0:T(8,128)S(1)} %own_rows.1.own, s32[16,128]{1,0:T(8,128)S(1)} %get-tuple-element.19.slot, f32[2,128,128]{2,1,0:T(8,128)S(1)} %bitcast.7), custom_call_target="tpu_custom_call" | custom-call | tf_op jit(solution)/shard_map/running_means/pallas_call | solution.py:289
Async XLA Ops:
  63.4 16.2 %all-to-all-start.3 = ((f32[8,136,128]{2,1,0:T(8,128)}), f32[8,136,128]{2,1,0:T(8,128)S(1)}, u32[]{:S(2)}, u32[]{:S(2)}) async-start(f32[8,136,128]{2,1,0:T(8,128)} %get-tuple-element.17), calls=%async_computation.3 | async-start | bytes 1114112 | tf_op jit(solution)/shard_map/all_to_all | solution.py:342
